TPU v7x, 512 devices: a whole 4x8x8 slice. The times are simulated.
512 devices in a mesh: cand: 8 (over x, core), blk: 8 (over z), feat: 8 (over y).
Axes of the slice: x: 4, y: 8, z: 8, core: 2. Of those that a mesh axis runs over, the one named last changes fastest.
Arguments:
- embeddings: float32 [131072, 1024], P(('cand', 'blk'), 'feat'), may hold values from -12 to 12
- winners: int32 [32, 3], replicated, may hold values from 0 to 131071, as said below
Outputs:
- columns: float32 [32, 3, 131072], P(None, None, ('cand', 'blk'))
- gains: float32 [32, 131072], P(None, ('cand', 'blk'))
- best: float32 [32, 3], replicated
Inputs may be any that keep to these rules, and one draw needn't show every extreme that they name: winners[b,k] lies in [k * 43690, (k + 1) * 43690), so the winners of a session are distinct.
All inputs are finite; a program needn't handle non-finite values.
Results may differ from a plain program's by a relative error of at most 0.00012.
Values sent between devices are 32-bit elements; how exact they have to be, the bound alone decides.
No kernel may reach another device: no remote copies, remote signals or barrier semaphores. Data moves between devices by JAX's collectives and lax.ppermute only.
A program may use at most 64 MiB of HBM per device.

v0:
```python
import functools

import jax
import jax.numpy as jnp
from jax import lax
from jax.sharding import Mesh
from jax.sharding import PartitionSpec as P

D = 1024
CAND_BLK = ("cand_0", "cand_1", "blk")


def by_axis(array, axes):
    return functools.reduce(lax.psum, axes, array)


def sent_to_all(array, axis):
    copies = jnp.broadcast_to(array, (lax.axis_size(axis), *array.shape))
    return lax.all_to_all(copies, axis, split_axis=0, concat_axis=0, tiled=True)


def over_copies(array, axis):
    everything = sent_to_all(array, axis)
    return jnp.sum(everything, axis=0)


def split_up(array, dim, devices):
    dims = array.shape
    pieces = array.reshape(*dims[:dim], devices, dims[dim] // devices, *dims[dim + 1 :])
    return jnp.moveaxis(pieces, dim, 0)


def sum_at_owner(array, axis, dim):
    devices = lax.axis_size(axis)
    pieces = lax.all_to_all(split_up(array, dim, devices), axis, 0, 0, tiled=True)
    return jnp.sum(pieces, axis=0)


def joined_along(pieces, dim):
    dims = list(pieces.shape[1:])
    dims[dim] *= pieces.shape[0]
    return jnp.moveaxis(pieces, 0, dim).reshape(dims)


def gather_directly(array, axis, dim):
    pieces = sent_to_all(array, axis)
    return joined_along(pieces, dim)


def of_everyone(array, axis):
    return sent_to_all(array, axis).max(axis=0)


def small_factor(gram_sum, norm_win):
    steps = gram_sum.shape[1]
    factor_rows = []
    radius_list = []
    for t in range(steps):
        carried = jnp.zeros_like(gram_sum[:, t, :])
        lowered = norm_win[:, t]
        for u in range(t):
            carried = carried + factor_rows[u][:, t : t + 1] * factor_rows[u]
            lowered = lowered - factor_rows[u][:, t] * factor_rows[u][:, t]
        radius = jnp.sqrt(jnp.maximum(lowered, 0.1))
        factor_rows.append((gram_sum[:, t, :] - carried) / radius[:, None])
        radius_list.append(radius)
    return (factor_rows, radius_list)


def columns_from(inner, factor_rows, radius_list):
    steps = inner.shape[1]
    finished = []
    for t in range(steps):
        carried = jnp.zeros_like(inner[:, t, :])
        for u in range(t):
            carried = carried + factor_rows[u][:, t : t + 1] * finished[u]
        finished.append((inner[:, t, :] - carried) / radius_list[t][:, None])
    return jnp.stack(finished, axis=1)


def batched_steps(embeddings, winners, positions, squared):
    rows_here = embeddings.shape[0]
    sessions = winners.shape[0]
    steps = winners.shape[1]
    chosen = winners.reshape(sessions * steps)
    onehot = (positions[None, :] == chosen[:, None]).astype(jnp.float32)
    row_part = jnp.dot(
        onehot, embeddings, precision=lax.Precision.HIGHEST, preferred_element_type=jnp.float32
    )
    norm_part = jnp.dot(
        onehot, squared, precision=lax.Precision.HIGHEST, preferred_element_type=jnp.float32
    )
    row_win, norm_win = (by_axis(row_part, CAND_BLK), by_axis(norm_part, CAND_BLK))
    partial_value = lax.dot_general(
        row_win,
        embeddings,
        (((1,), (1,)), ((), ())),
        precision=lax.Precision.HIGHEST,
        preferred_element_type=jnp.float32,
    )
    partial_value = partial_value.reshape(sessions, steps, rows_here)
    row_set = row_win.reshape(sessions, steps, row_win.shape[1])
    gram_part = jnp.einsum("bsf,btf->bst", row_set, row_set, precision=lax.Precision.HIGHEST)
    norm_win = norm_win.reshape(sessions, steps)
    gram_sum = over_copies(gram_part, "feat")
    inner_share = sum_at_owner(partial_value, "feat", 2) / D
    factor_rows, radius_list = small_factor(gram_sum / D, norm_win)
    col_share = columns_from(inner_share, factor_rows, radius_list)
    return gather_directly(col_share, "feat", 2)


def body(embeddings, winners):
    rows_here = embeddings.shape[0]
    sessions = winners.shape[0]
    steps = winners.shape[1]
    offset = lax.axis_index(CAND_BLK) * rows_here
    positions = offset + jnp.arange(rows_here, dtype=jnp.int32)
    squared = over_copies(jnp.sum(embeddings * embeddings, axis=1), "feat") / D
    columns = batched_steps(embeddings, winners, positions, squared)
    gains = jnp.broadcast_to(squared[None, :], (sessions, rows_here))
    maxima = []
    for k in range(steps):
        maxima.append(jnp.max(gains, axis=1))
        gains = gains - columns[:, k, :] * columns[:, k, :]
    best = of_everyone(jnp.stack(maxima, axis=1), CAND_BLK)
    return (columns, gains, best)


def solution(mesh):
    torus = Mesh(
        mesh.devices.reshape(4, 2, mesh.shape["blk"], mesh.shape["feat"]),
        ("cand_0", "cand_1", "blk", "feat"),
    )
    placed = (P(CAND_BLK, "feat"), P())
    return jax.shard_map(
        body,
        mesh=torus,
        in_specs=placed,
        out_specs=(P(None, None, CAND_BLK), P(None, CAND_BLK), P()),
        check_vma=False,
    )
```

profile of v0, /device:TPU:1, one launch (start us, length us, event | category | flops | bytes accessed | tf_op | source)
XLA Modules:
  0.0 147.3 jit_solution(11687453908426175664)
XLA Ops:
  0.6 1.7 %multiply_reduce_fusion = f32[2048]{0:T(1024)S(1)} fusion(f32[2048,128]{1,0:T(8,128)} %param.2), kind=kLoop, calls=%fused_computation.1 | loop fusion | flops 522240 | bytes 1056768 | tf_op jit(solution)/shard_map/reduce_sum | solution.py:118
  2.3 0.7 broadcast_in_dim.10
  3.0 7.6 %all-to-all-start.1 = ((f32[8,1,2048]{2,1,0:T(1,128)}), f32[8,1,2048]{2,1,0:T(1,128)S(1)}, u32[]{:S(2)}, u32[]{:S(2)}) async-start(f32[8,1,2048]{2,1,0:T(1,128)} %broadcast_in_dim.10), calls=%async_computation.1 | async-start | bytes 131072 | tf_op jit(solution)/shard_map/all_to_all | solution.py:19
  10.6 0.7 copy-done.2
  11.4 0.1 eq.16
  11.5 0.7 fusion.1
  12.1 5.7 %all-to-all-done.1 = f32[8,1,2048]{2,1,0:T(1,128)S(1)} async-done(((f32[8,1,2048]{2,1,0:T(1,128)}), f32[8,1,2048]{2,1,0:T(1,128)S(1)}, u32[]{:S(2)}, u32[]{:S(2)}) %all-to-all-start.1) | async-done | bytes 65568 | tf_op jit(solution)/shard_map/all_to_all | solution.py:19
  17.9 0.6 fusion.20
  18.5 0.5 convolution_bitcast_fusion
  19.0 13.8 %all-reduce.1 = (f32[96,128]{1,0:T(8,128)S(1)}, f32[96]{0:T(128)S(1)}) all-reduce(f32[96,128]{1,0:T(8,128)S(1)} %fusion.1, f32[96]{0:T(128)S(1)} %convolution_bitcast_fusion), channel_id=1, replica_groups=mesh['cand_0'=4,'cand_1'=2,'blk'=8,'feat'=8] {'cand_0'}, use_global_device_ids=true, to_apply=%region_0.0 | all-reduce | flops 12384 | bytes 99072 | tf_op jit(solution)/shard_map/psum | solution.py:14
  32.8 9.2 %all-reduce.2 = (f32[96,128]{1,0:T(8,128)S(1)}, f32[96]{0:T(128)S(1)}) all-reduce(f32[96,128]{1,0:T(8,128)S(1)} %get-tuple-element.7, f32[96]{0:T(128)S(1)} %get-tuple-element.8), channel_id=1, replica_groups=mesh['cand_0'=4,'cand_1'=2,'blk'=8,'feat'=8] {'cand_1'}, use_global_device_ids=true, to_apply=%region_1.0 | all-reduce | flops 12384 | bytes 99072 | tf_op jit(solution)/shard_map/psum | solution.py:14
  42.0 0.1 reshape.90
  42.2 29.3 %all-reduce = (f32[96,128]{1,0:T(8,128)S(1)}, f32[32,3]{0,1:T(4,128)S(1)}) all-reduce(f32[96,128]{1,0:T(8,128)S(1)} %get-tuple-element.9, f32[32,3]{0,1:T(4,128)S(1)} %copy.58), channel_id=1, replica_groups=mesh['cand_0'=4,'cand_1'=2,'blk'=8,'feat'=8] {'blk'}, use_global_device_ids=true, to_apply=%region_2.0 | all-reduce | flops 12384 | bytes 99072 | tf_op jit(solution)/shard_map/psum | solution.py:14
  71.6 0.3 fusion.23
  72.0 0.7 reshape.96
  72.7 3.3 %all-to-all-start.2 = ((f32[8,1,288]{2,1,0:T(1,128)}), f32[8,1,288]{2,1,0:T(1,128)S(1)}, u32[]{:S(2)}, u32[]{:S(2)}) async-start(f32[8,1,288]{2,1,0:T(1,128)} %reshape.96), calls=%async_computation.2 | async-start | bytes 24576 | tf_op jit(solution)/shard_map/all_to_all | solution.py:19
  76.1 1.2 fusion.22
  77.2 0.2 copy.64
  77.5 1.1 copy.66
  78.6 4.0 %all-to-all-done.2 = f32[8,1,288]{2,1,0:T(1,128)S(1)} async-done(((f32[8,1,288]{2,1,0:T(1,128)}), f32[8,1,288]{2,1,0:T(1,128)S(1)}, u32[]{:S(2)}, u32[]{:S(2)}) %all-to-all-start.2) | async-done | bytes 9248 | tf_op jit(solution)/shard_map/all_to_all | solution.py:19
  82.6 3.5 %all-to-all-start = ((f32[8,32,3,256]{3,1,2,0:T(8,128)}), f32[8,32,3,256]{3,1,2,0:T(8,128)S(1)}, u32[]{:S(2)}, u32[]{:S(2)}) async-start(f32[8,32,3,256]{3,1,2,0:T(8,128)} %bitcast.72), calls=%async_computation | async-start | bytes 1572864 | tf_op jit(solution)/shard_map/all_to_all | solution.py:35
  86.2 0.5 broadcast.69
  86.7 0.7 reduce.4
  87.6 13.7 %all-to-all-done = f32[8,32,3,256]{3,1,2,0:T(8,128)S(1)} async-done(((f32[8,32,3,256]{3,1,2,0:T(8,128)}), f32[8,32,3,256]{3,1,2,0:T(8,128)S(1)}, u32[]{:S(2)}, u32[]{:S(2)}) %all-to-all-start) | async-done | bytes 786464 | tf_op jit(solution)/shard_map/all_to_all | solution.py:35
  101.3 0.1 fusion.15
  101.4 1.0 broadcast_in_dim.12
  102.4 3.5 %all-to-all-start.3 = ((f32[8,32,3,256]{3,1,2,0:T(8,128)}), f32[8,32,3,256]{3,1,2,0:T(8,128)S(1)}, u32[]{:S(2)}, u32[]{:S(2)}) async-start(f32[8,32,3,256]{3,1,2,0:T(8,128)} %broadcast_in_dim.12), calls=%async_computation.3 | async-start | bytes 1572864 | tf_op jit(solution)/shard_map/all_to_all | solution.py:19
  106.0 0.7 pad.clone
  106.6 14.3 %all-to-all-done.3 = f32[8,32,3,256]{3,1,2,0:T(8,128)S(1)} async-done(((f32[8,32,3,256]{3,1,2,0:T(8,128)}), f32[8,32,3,256]{3,1,2,0:T(8,128)S(1)}, u32[]{:S(2)}, u32[]{:S(2)}) %all-to-all-start.3) | async-done | bytes 786464 | tf_op jit(solution)/shard_map/all_to_all | solution.py:19
  121.0 1.0 fusion.13
  122.1 24.6 %all_to_all.26 = f32[64,32,3]{1,2,0:T(4,128)S(1)} all-to-all(f32[64,32,3]{1,2,0:T(4,128)S(1)} %broadcast_in_dim.28), channel_id=1, replica_groups=mesh['cand_0'=4,'cand_1'=2,'blk'=8,'feat'=8] {'cand_0','cand_1','blk'}, dimensions={0} | all-to-all | bytes 49152 | tf_op jit(solution)/shard_map/all_to_all | solution.py:19
  146.6 0.7 reduce_max.39
  (26 shorter events, 0.8 us)
Async XLA Ops:
  0.6 10.9 %copy-start = (f32[2048,128]{1,0:T(8,128)S(1)}, f32[2048,128]{1,0:T(8,128)}, u32[]{:S(2)}) copy-start(f32[2048,128]{1,0:T(8,128)} %param.2) | copy-start | bytes 3145732
  3.0 14.9 %all-to-all-start.1 = ((f32[8,1,2048]{2,1,0:T(1,128)}), f32[8,1,2048]{2,1,0:T(1,128)S(1)}, u32[]{:S(2)}, u32[]{:S(2)}) async-start(f32[8,1,2048]{2,1,0:T(1,128)} %broadcast_in_dim.10), calls=%async_computation.1 | async-start | bytes 131072 | tf_op jit(solution)/shard_map/all_to_all | solution.py:19
  10.6 0.7 copy-start.2
  72.7 9.9 %all-to-all-start.2 = ((f32[8,1,288]{2,1,0:T(1,128)}), f32[8,1,288]{2,1,0:T(1,128)S(1)}, u32[]{:S(2)}, u32[]{:S(2)}) async-start(f32[8,1,288]{2,1,0:T(1,128)} %reshape.96), calls=%async_computation.2 | async-start | bytes 24576 | tf_op jit(solution)/shard_map/all_to_all | solution.py:19
  82.6 18.6 %all-to-all-start = ((f32[8,32,3,256]{3,1,2,0:T(8,128)}), f32[8,32,3,256]{3,1,2,0:T(8,128)S(1)}, u32[]{:S(2)}, u32[]{:S(2)}) async-start(f32[8,32,3,256]{3,1,2,0:T(8,128)} %bitcast.72), calls=%async_computation | async-start | bytes 1572864 | tf_op jit(solution)/shard_map/all_to_all | solution.py:35
  102.4 18.5 %all-to-all-start.3 = ((f32[8,32,3,256]{3,1,2,0:T(8,128)}), f32[8,32,3,256]{3,1,2,0:T(8,128)S(1)}, u32[]{:S(2)}, u32[]{:S(2)}) async-start(f32[8,32,3,256]{3,1,2,0:T(8,128)} %broadcast_in_dim.12), calls=%async_computation.3 | async-start | bytes 1572864 | tf_op jit(solution)/shard_map/all_to_all | solution.py:19
  121.0 26.3 %copy-start.1 = (f32[8,3,4,8,256]{4,3,0,2,1:T(8,128)}, f32[8,3,4,8,256]{4,3,0,2,1:T(8,128)S(1)}, u32[]{:S(2)}) copy-start(f32[8,3,4,8,256]{4,3,0,2,1:T(8,128)S(1)} %copy.63) | copy-start | bytes 2359300
where the time goes:
time: 148 us; the launch traced here: 147 us
  blocking collectives  76.9 us (52%)
  waiting for transfers between devices  37.6 us (25%)
  starting transfers between devices  18.1 us (12%)
  local copies, waits for them, and re-layouts  6.22 us (4%)
  other arithmetic  4.93 us (3%)
  matrix products  2.66 us (2%)
    psum x3, blocking collectives, by_axis(): return functools.reduce(lax.psum, axes, array)  52.3 us
    all_to_all x1, blocking collectives, sent_to_all(): return lax.all_to_all(copies, axis, split_axis=0, concat_axis=0, tiled=True)  24.6 us
    all_to_all x3, waiting for transfers between devices, sent_to_all(): return lax.all_to_all(copies, axis, split_axis=0, concat_axis=0, tiled=True)  24 us
    all_to_all x3, starting transfers between devices, sent_to_all(): return lax.all_to_all(copies, axis, split_axis=0, concat_axis=0, tiled=True)  14.5 us
    all_to_all x1, waiting for transfers between devices, sum_at_owner(): lax.all_to_all(split_up(array, dim, devices), axis, 0, 0, tiled=True)  13.7 us
    all_to_all x1, starting transfers between devices, sum_at_owner(): lax.all_to_all(split_up(array, dim, devices), axis, 0, 0, tiled=True)  3.55 us
  transfers between devices with their start and end apart: 4, of which 4 were waited for; matrix products, arithmetic and copies ran while one was open for 4% of the time, Pallas kernels for 0%

commit v1 on v0

v1 whole, which is shorter than its diff:
```python
import jax
import jax.numpy as jnp
from jax import lax
from jax.experimental import pallas as pl
from jax.experimental.pallas import tpu as pltpu
from jax.sharding import Mesh
from jax.sharding import PartitionSpec as P

D = 1024
CANDS = 131072
SESSIONS = 32
STEPS = 3
LANES = 128
PICKS = STEPS * SESSIONS
FLOOR = 0.1
CAND = ("cand_0", "cand_1")
CAND_BLK = ("cand_0", "cand_1", "blk")
FEAT = ("feat_hi", "feat_lo")
EXACT = lax.Precision.HIGHEST
PAIRS = [(t, u) for t in range(STEPS) for u in range(t, STEPS)]
VMEM = pl.BlockSpec(memory_space=pltpu.VMEM)


def share_with(array, axes):
    devices = lax.axis_size(axes)
    copies = jnp.broadcast_to(array, (devices, *array.shape))
    return lax.all_to_all(copies, axes, 0, 0, tiled=True)


def first_step(group, groups):
    return min(group * (CANDS // groups) // (CANDS // STEPS), STEPS - 2)


def winner_rows(embeddings, winners):
    rows_here, width = embeddings.shape
    groups = lax.axis_size(CAND)
    turn = [first_step(g, groups) for g in range(groups)].index(1)
    late = lax.axis_index(CAND) >= turn
    offset = lax.axis_index(CAND_BLK) * rows_here
    by_step = winners.T
    chosen = jnp.where(late, by_step[1:], by_step[:2]).reshape(2 * SESSIONS)
    positions = offset + jnp.arange(rows_here, dtype=jnp.int32)
    onehot = (positions[None, :] == chosen[:, None]).astype(jnp.float32)
    part = jnp.dot(onehot, embeddings, precision=EXACT, preferred_element_type=jnp.float32)
    group_rows = jnp.sum(share_with(part, "blk"), axis=0)
    spread = share_with(group_rows, (*CAND, "feat_lo"))
    spread = spread.reshape(groups, 2, 2, SESSIONS, width)
    low = jnp.sum(spread[:turn], axis=0)
    high = jnp.sum(spread[turn:], axis=0)
    rows = jnp.stack([low[:, 0], low[:, 1] + high[:, 0], high[:, 1]], axis=1)
    return rows.reshape(2, PICKS, width)


def times_rows(left, right):
    return lax.dot_general(
        left, right, (((1,), (1,)), ((), ())), precision=EXACT, preferred_element_type=jnp.float32
    )


def in_rows(tiles):
    at = lax.broadcasted_iota(jnp.int32, (8, LANES), 0)
    tile = jnp.zeros((8, LANES), jnp.float32)
    for row, values in enumerate(tiles):
        tile = jnp.where(at == row, jnp.broadcast_to(values[:1], (8, LANES)), tile)
    return tile


def products_kernel(rows_ref, other_rows_ref, mine_ref, got_ref, out_ref):
    ones = jnp.ones((8, LANES), jnp.float32)
    rows, other_rows = rows_ref[...], other_rows_ref[...]
    crossed = jnp.concatenate(
        [
            rows[t * SESSIONS : (t + 1) * SESSIONS] * rows[u * SESSIONS : (u + 1) * SESSIONS]
            + other_rows[t * SESSIONS : (t + 1) * SESSIONS] * other_rows[u * SESSIONS : (u + 1) * SESSIONS]
            for t, u in PAIRS
        ]
        + [jnp.zeros((2 * LANES - len(PAIRS) * SESSIONS, LANES), jnp.float32)]
    )
    gram = times_rows(ones, crossed)
    for q in range(out_ref.shape[0]):
        norms = []
        for h in range(2):
            at = pl.ds((2 * q + h) * LANES, LANES)
            mine, got = mine_ref[at, :], got_ref[at, :]
            out_ref[q, pl.ds(h * PICKS, PICKS), :] = times_rows(rows, mine) + times_rows(other_rows, got)
            norms.append(times_rows(ones, mine * mine + got * got))
        out_ref[q, pl.ds(2 * PICKS, 8), :] = in_rows([*norms, gram[:, :LANES], gram[:, LANES:]])


def columns_kernel(parts_ref, out_ref):
    total = parts_ref[0]
    for q in range(1, parts_ref.shape[0]):
        total = total + parts_ref[q]
    total = total * (1.0 / D)
    session = lax.broadcasted_iota(jnp.int32, (SESSIONS, LANES), 0)
    lane = lax.broadcasted_iota(jnp.int32, (SESSIONS, LANES), 1)
    gram = {}
    for i, pair in enumerate(PAIRS):
        row = total[2 * PICKS + 2 + i // 4 : 2 * PICKS + 3 + i // 4]
        picked = jnp.where(lane == (i % 4) * SESSIONS + session, jnp.broadcast_to(row, session.shape), 0.0)
        gram[pair] = jnp.sum(picked, axis=1, keepdims=True)
    factor, radius = {}, []
    for k in range(STEPS):
        left = gram[k, k]
        for t in range(k):
            left = left - factor[t, k] * factor[t, k]
        radius.append(jnp.sqrt(jnp.maximum(left, FLOOR)))
        for u in range(k + 1, STEPS):
            rest = gram[k, u]
            for t in range(k):
                rest = rest - factor[t, k] * factor[t, u]
            factor[k, u] = rest / radius[k]
    blocks, norms, tops = [], [], [[], []]
    for h in range(2):
        norm = total[2 * PICKS + h : 2 * PICKS + h + 1]
        norms.append(norm)
        gains = jnp.broadcast_to(norm, (SESSIONS, LANES))
        columns = []
        for k in range(STEPS):
            start = h * PICKS + k * SESSIONS
            column = total[start : start + SESSIONS]
            for t in range(k):
                column = column - factor[t, k] * columns[t]
            column = column / radius[k]
            columns.append(column)
            if k < STEPS - 1:
                gains = gains - column * column
                tops[k].append(jnp.max(gains, axis=1, keepdims=True))
        blocks += columns
    first = jnp.max(jnp.maximum(norms[0], norms[1]), axis=1, keepdims=True)
    maxima = [jnp.broadcast_to(first, (SESSIONS, 1))] + [jnp.maximum(*pair) for pair in tops]
    best = jnp.zeros((1, LANES), jnp.float32)
    for k, values in enumerate(maxima):
        placed = jnp.where(lane == k * SESSIONS + session, jnp.broadcast_to(values, session.shape), 0.0)
        best = best + jnp.sum(placed, axis=0, keepdims=True)
    whole = jnp.concatenate([*blocks, in_rows([*norms, best])])
    for f in range(out_ref.shape[0]):
        out_ref[f] = whole


def results_kernel(spread_ref, columns_ref, gains_ref):
    his = spread_ref.shape[0] // 2
    for f in range(2 * his):
        for h in range(2):
            at = pl.ds(((f % 2) * his + f // 2) * 2 * LANES + h * LANES, LANES)
            gains = jnp.broadcast_to(spread_ref[f, pl.ds(2 * PICKS + h, 1), :], (SESSIONS, LANES))
            for k in range(STEPS):
                column = spread_ref[f, pl.ds(h * PICKS + k * SESSIONS, SESSIONS), :]
                columns_ref[k, :, at] = column
                gains = gains - column * column
            gains_ref[:, at] = gains


def selection(embeddings, winners):
    rows_here, _ = embeddings.shape
    his, half = lax.axis_size("feat_hi"), rows_here // 2
    side = lax.axis_index("feat_lo")
    mine = lax.dynamic_slice_in_dim(embeddings, side * half, half)
    other = lax.dynamic_slice_in_dim(embeddings, (1 - side) * half, half)
    got = lax.ppermute(other, "feat_lo", [(0, 1), (1, 0)])
    rows = winner_rows(embeddings, winners)
    own_rows = jnp.where(side == 0, rows[0], rows[1])
    other_rows = jnp.where(side == 0, rows[1], rows[0])
    piece = (2 * PICKS + 8, LANES)
    products = pl.pallas_call(
        products_kernel,
        out_shape=jax.ShapeDtypeStruct((his, *piece), jnp.float32),
        in_specs=[VMEM] * 4,
        out_specs=VMEM,
        cost_estimate=pl.CostEstimate(flops=2 * PICKS * half * 256, bytes_accessed=2 << 20, transcendentals=0),
    )(own_rows, other_rows, mine, got)
    parts = lax.all_to_all(products, "feat_hi", 0, 0, tiled=True)
    share = pl.pallas_call(
        columns_kernel,
        out_shape=jax.ShapeDtypeStruct((2 * his, *piece), jnp.float32),
        in_specs=[VMEM],
        out_specs=VMEM,
        cost_estimate=pl.CostEstimate(flops=1 << 20, bytes_accessed=2 << 20, transcendentals=0),
    )(parts)
    spread = lax.all_to_all(share, FEAT, 0, 0, tiled=True)
    tops = jnp.max(spread[:, 2 * PICKS + 2, :], axis=0)
    best = share_with(tops.reshape(1, LANES), CAND_BLK).max(axis=(0, 1))
    best = best[:PICKS].reshape(STEPS, SESSIONS).T
    columns, gains = pl.pallas_call(
        results_kernel,
        out_shape=(
            jax.ShapeDtypeStruct((STEPS, SESSIONS, rows_here), jnp.float32),
            jax.ShapeDtypeStruct((SESSIONS, rows_here), jnp.float32),
        ),
        in_specs=[VMEM],
        out_specs=(VMEM, VMEM),
        cost_estimate=pl.CostEstimate(flops=1 << 20, bytes_accessed=2 << 20, transcendentals=0),
    )(spread)
    return (columns.transpose(1, 0, 2), gains, best)


def solution(mesh):
    torus = Mesh(
        mesh.devices.reshape(4, 2, mesh.shape["blk"], mesh.shape["feat"] // 2, 2),
        ("cand_0", "cand_1", "blk", "feat_hi", "feat_lo"),
    )
    return jax.shard_map(
        selection,
        mesh=torus,
        in_specs=(P(CAND_BLK, FEAT), P()),
        out_specs=(P(None, None, CAND_BLK), P(None, CAND_BLK), P()),
        check_vma=False,
    )
```

time: 148 us -> 124 us (0.84)
  waiting for transfers between devices: 37.6 us -> 21.2 us
  blocking collectives: 76.9 us -> 64.4 us
  Pallas kernels: 0 us -> 9.26 us
  other arithmetic: 4.93 us -> 0.79 us
  starting transfers between devices: 18.1 us -> 20.1 us
  local copies, waits for them, and re-layouts: 6.22 us -> 4.68 us
    psum x3 -> x0, blocking collectives: 52.3 us -> none  [by_axis(): return functools.reduce(lax.psum, axes, array)]
    all_to_all x1 -> x3, blocking collectives: 24.6 us -> 64.4 us  [the longest x1 25 us: selection(): spread = lax.all_to_all(share, FEAT, 0, 0, tiled=True)]
    all_to_all x4 -> x2, waiting for transfers between devices: 37.6 us -> 12.5 us  [share_with(): return lax.all_to_all(copies, axes, 0, 0, tiled=True)]
    pallas_call x0 -> x3, Pallas kernels: none -> 9.26 us  [the longest x1 4.96 us: selection(): pl.pallas_call(products_kernel, out_shape=jax.ShapeDtypeStruct((his, *pie...]
    ppermute x0 -> x1, waiting for transfers between devices: none -> 8.66 us  [selection(): got = lax.ppermute(other, 'feat_lo', [(0, 1), (1, 0)])]
    ppermute x0 -> x1, starting transfers between devices: none -> 3.25 us  [selection(): got = lax.ppermute(other, 'feat_lo', [(0, 1), (1, 0)])]
    reduce_max x3 -> x2, other arithmetic: 2.22 us -> 0.05 us  [the longest x1 0.03 us: selection(): tops = jnp.max(spread[:, 2 * PICKS + 2, :], axis=0)]
    another operation x2 -> x0, local copies, waits for them, and re-layouts: 1.77 us -> none  [the longest x1 1.12 us: split_up(): array.reshape(*dims[:dim], devices, dims[dim] // devices, *dims[dim + 1:])]
  transfers between devices with their start and end apart: 4 -> 3, of which waited for: 4 -> 3; matrix products, arithmetic and copies ran while one was open for 4% -> 1% of each run, Pallas kernels for 0% -> 2%
where the time goes in v1:
time: 124 us; the launch traced here: 123 us
  blocking collectives  64.4 us (52%)
  waiting for transfers between devices  21.2 us (17%)
  starting transfers between devices  20.1 us (16%)
  Pallas kernels  9.26 us (7%)
  local copies, waits for them, and re-layouts  4.68 us (4%)
  matrix products  1.76 us (1%)
    all_to_all x1, blocking collectives, selection(): spread = lax.all_to_all(share, FEAT, 0, 0, tiled=True)  25 us
    all_to_all x1, blocking collectives, share_with(): return lax.all_to_all(copies, axes, 0, 0, tiled=True)  21.1 us
    all_to_all x1, blocking collectives, selection(): parts = lax.all_to_all(products, 'feat_hi', 0, 0, tiled=True)  18.3 us
    all_to_all x2, starting transfers between devices, share_with(): return lax.all_to_all(copies, axes, 0, 0, tiled=True)  16.8 us
    all_to_all x2, waiting for transfers between devices, share_with(): return lax.all_to_all(copies, axes, 0, 0, tiled=True)  12.5 us
    ppermute x1, waiting for transfers between devices, selection(): got = lax.ppermute(other, 'feat_lo', [(0, 1), (1, 0)])  8.66 us
    pallas_call x1, Pallas kernels, selection(): pl.pallas_call(products_kernel, out_shape=jax.ShapeDtypeStruct((his, *pie...  4.96 us
    ppermute x1, starting transfers between devices, selection(): got = lax.ppermute(other, 'feat_lo', [(0, 1), (1, 0)])  3.25 us
  transfers between devices with their start and end apart: 3, of which 3 were waited for; matrix products, arithmetic and copies ran while one was open for 1% of the time, Pallas kernels for 2%

profile of v1, /device:TPU:1, one launch (start us, length us, event | category | flops | bytes accessed | tf_op | source)
XLA Modules:
  0.0 122.9 jit_solution(8820146482525496635)
XLA Ops:
  0.7 0.0 copy-start.3
  0.7 0.7 copy-done.3
  1.4 0.1 eq.21
  1.4 1.8 %fusion = f32[64,128]{1,0:T(8,128)S(1)} fusion(f32[2048,128]{1,0:T(8,128)} %param.2, s32[2048]{0:T(1024)S(1)} %iota_add_fusion, s32[64]{0:T(128)S(1)} %eq.21), kind=kOutput, calls=%fused_computation | convolution fusion | flops 201457664 | bytes 1089792 | tf_op jit(solution)/shard_map/dot_general | solution.py:44
  3.2 21.1 %all_to_all.25 = f32[8,64,128]{2,1,0:T(8,128)S(1)} all-to-all(f32[8,64,128]{2,1,0:T(8,128)S(1)} %broadcast_in_dim.10), channel_id=1, replica_groups=mesh['cand_0'=4,'cand_1'=2,'blk'=8,'feat_hi'=4,'feat_lo'=2] {'blk'}, dimensions={0} | all-to-all | bytes 524288 | tf_op jit(solution)/shard_map/all_to_all | solution.py:27
  24.4 0.0 copy-start
  24.4 0.8 broadcast_in_dim.11
  25.2 7.7 %all-to-all-start.1 = ((f32[16,64,128]{2,1,0:T(8,128)}), f32[16,64,128]{2,1,0:T(8,128)S(1)}, u32[]{:S(2)}, u32[]{:S(2)}) async-start(f32[16,64,128]{2,1,0:T(8,128)} %broadcast_in_dim.11), calls=%async_computation.1 | async-start | bytes 1048576 | tf_op jit(solution)/shard_map/all_to_all | solution.py:27
  32.9 0.0 copy-done
  32.9 0.9 constant_dynamic-slice_fusion
  33.8 3.2 %collective-permute-start = (f32[1024,128]{1,0:T(8,128)S(1)}, f32[1024,128]{1,0:T(8,128)S(1)}, u32[]{:S(2)}, u32[]{:S(2)}) collective-permute-start(f32[1024,128]{1,0:T(8,128)S(1)} %get-tuple-element.7), channel_id=1, source_target_pairs={{0,1},{1,0},{2,3},{3,2},{4,5},{5,4},{6,7},{7,6},{8,9},{9,8},{10,11... | collective-permute-start | bytes 1572872 | tf_op jit(solution)/shard_map/ppermute | solution.py:160
  37.0 5.5 %all-to-all-done.1 = f32[16,64,128]{2,1,0:T(8,128)S(1)} async-done(((f32[16,64,128]{2,1,0:T(8,128)}), f32[16,64,128]{2,1,0:T(8,128)S(1)}, u32[]{:S(2)}, u32[]{:S(2)}) %all-to-all-start.1) | async-done | bytes 524320 | tf_op jit(solution)/shard_map/all_to_all | solution.py:27
  42.7 0.6 slice_select_fusion
  43.3 8.7 %collective-permute-done.got_ref = f32[1024,128]{1,0:T(8,128)S(1)} collective-permute-done((f32[1024,128]{1,0:T(8,128)S(1)}, f32[1024,128]{1,0:T(8,128)S(1)}, u32[]{:S(2)}, u32[]{:S(2)}) %collective-permute-start) | collective-permute-done | bytes 524320 | tf_op jit(solution)/shard_map/ppermute | solution.py:160
  52.0 0.0 copy-start.2
  52.0 0.8 copy-done.2
  52.8 5.0 %shard_map.49 = f32[4,200,128]{2,1,0:T(8,128)} custom-call(f32[96,128]{1,0:T(8,128)} %bitcast.13, f32[96,128]{1,0:T(8,128)} %bitcast.12, f32[1024,128]{1,0:T(8,128)} %get-tuple-element.8.mine_ref, f32[1024,128]{1,0:T(8,128)} %copy-done.2), custom_call_target="tpu_custom_call" | custom-call | flops 50331648 | bytes 2097152 | tf_op jit(solution)/shard_map/pallas_call | solution.py:165
  57.7 18.3 %all_to_all.26.parts_ref = f32[4,200,128]{2,1,0:T(8,128)} all-to-all(f32[4,200,128]{2,1,0:T(8,128)} %shard_map.49), channel_id=1, replica_groups=mesh['cand_0'=4,'cand_1'=2,'blk'=8,'feat_hi'=4,'feat_lo'=2] {'feat_hi'}, dimensions={0} | all-to-all | bytes 819200 | tf_op jit(solution)/shard_map/all_to_all | solution.py:172
  76.0 2.1 %shard_map.50 = f32[8,200,128]{2,1,0:T(8,128)} custom-call(f32[4,200,128]{2,1,0:T(8,128)} %all_to_all.26.parts_ref), custom_call_target="tpu_custom_call" | custom-call | flops 1048576 | bytes 2097152 | tf_op jit(solution)/shard_map/pallas_call | solution.py:173
  78.1 25.0 %all_to_all.27.spread_ref = f32[8,200,128]{2,1,0:T(8,128)S(1)} all-to-all(f32[8,200,128]{2,1,0:T(8,128)} %shard_map.50), channel_id=1, replica_groups=mesh['cand_0'=4,'cand_1'=2,'blk'=8,'feat_hi'=4,'feat_lo'=2] {'feat_hi','..., dimensions={0} | all-to-all | bytes 1638400 | tf_op jit(solution)/shard_map/all_to_all | solution.py:180
  103.1 0.0 copy-start.1
  103.1 0.7 broadcast_in_dim.12
  103.8 9.2 %all-to-all-start.4 = ((f32[64,1,128]{2,1,0:T(1,128)}), f32[64,1,128]{2,1,0:T(1,128)S(1)}, u32[]{:S(2)}, u32[]{:S(2)}) async-start(f32[64,1,128]{2,1,0:T(1,128)} %broadcast_in_dim.12), calls=%async_computation.4 | async-start | bytes 65536 | tf_op jit(solution)/shard_map/all_to_all | solution.py:27
  113.0 0.0 copy-done.1
  113.0 2.2 %shard_map.51 = (f32[3,32,2048]{2,1,0:T(8,128)}, f32[32,2048]{1,0:T(8,128)}) custom-call(f32[8,200,128]{2,1,0:T(8,128)} %copy-done.1), custom_call_target="tpu_custom_call" | custom-call | flops 1048576 | bytes 2097152 | tf_op jit(solution)/shard_map/pallas_call | solution.py:184
  115.2 7.0 %all-to-all-done.4 = f32[64,1,128]{2,1,0:T(1,128)S(1)} async-done(((f32[64,1,128]{2,1,0:T(1,128)}), f32[64,1,128]{2,1,0:T(1,128)S(1)}, u32[]{:S(2)}, u32[]{:S(2)}) %all-to-all-start.4) | async-done | bytes 32800 | tf_op jit(solution)/shard_map/all_to_all | solution.py:27
  122.2 0.7 reshape.35
  (12 shorter events, 0.2 us)
Async XLA Ops:
  0.7 0.7 copy-start.3
  24.4 8.5 %copy-start = (f32[2048,128]{1,0:T(8,128)S(1)}, f32[2048,128]{1,0:T(8,128)}, u32[]{:S(2)}) copy-start(f32[2048,128]{1,0:T(8,128)} %param.2) | copy-start | bytes 3145732
  25.2 17.3 %all-to-all-start.1 = ((f32[16,64,128]{2,1,0:T(8,128)}), f32[16,64,128]{2,1,0:T(8,128)S(1)}, u32[]{:S(2)}, u32[]{:S(2)}) async-start(f32[16,64,128]{2,1,0:T(8,128)} %broadcast_in_dim.11), calls=%async_computation.1 | async-start | bytes 1048576 | tf_op jit(solution)/shard_map/all_to_all | solution.py:27
  33.8 18.2 %collective-permute-start = (f32[1024,128]{1,0:T(8,128)S(1)}, f32[1024,128]{1,0:T(8,128)S(1)}, u32[]{:S(2)}, u32[]{:S(2)}) collective-permute-start(f32[1024,128]{1,0:T(8,128)S(1)} %get-tuple-element.7), channel_id=1, source_target_pairs={{0,1},{1,0},{2,3},{3,2},{4,5},{5,4},{6,7},{7,6},{8,9},{9,8},{10,11... | collective-permute-start | bytes 1572872 | tf_op jit(solution)/shard_map/ppermute | solution.py:160
  52.0 0.8 copy-start.2
  103.1 9.9 %copy-start.1 = (f32[8,200,128]{2,1,0:T(8,128)}, f32[8,200,128]{2,1,0:T(8,128)S(1)}, u32[]{:S(2)}) copy-start(f32[8,200,128]{2,1,0:T(8,128)S(1)} %all_to_all.27.spread_ref) | copy-start | bytes 2457604
  103.8 18.4 %all-to-all-start.4 = ((f32[64,1,128]{2,1,0:T(1,128)}), f32[64,1,128]{2,1,0:T(1,128)S(1)}, u32[]{:S(2)}, u32[]{:S(2)}) async-start(f32[64,1,128]{2,1,0:T(1,128)} %broadcast_in_dim.12), calls=%async_computation.4 | async-start | bytes 65536 | tf_op jit(solution)/shard_map/all_to_all | solution.py:27

commit v2 on v1

--- a/solution.py
+++ b/solution.py
@@ -5,6 +5,7 @@
 from jax.experimental.pallas import tpu as pltpu
 from jax.sharding import Mesh
 from jax.sharding import PartitionSpec as P
+
 
 D = 1024
 CANDS = 131072
@@ -19,6 +20,7 @@
 EXACT = lax.Precision.HIGHEST
 PAIRS = [(t, u) for t in range(STEPS) for u in range(t, STEPS)]
 VMEM = pl.BlockSpec(memory_space=pltpu.VMEM)
+PARAMS = pltpu.CompilerParams(vmem_limit_bytes=12 << 20)
 
 
 def share_with(array, axes):
@@ -66,25 +68,33 @@
 
 
 def products_kernel(rows_ref, other_rows_ref, mine_ref, got_ref, out_ref):
-    ones = jnp.ones((8, LANES), jnp.float32)
+    step = lax.broadcasted_iota(jnp.int32, (SESSIONS, LANES), 0)
+    lane = lax.broadcasted_iota(jnp.int32, (SESSIONS, LANES), 1)
     rows, other_rows = rows_ref[...], other_rows_ref[...]
-    crossed = jnp.concatenate(
-        [
-            rows[t * SESSIONS : (t + 1) * SESSIONS] * rows[u * SESSIONS : (u + 1) * SESSIONS]
-            + other_rows[t * SESSIONS : (t + 1) * SESSIONS] * other_rows[u * SESSIONS : (u + 1) * SESSIONS]
-            for t, u in PAIRS
-        ]
-        + [jnp.zeros((2 * LANES - len(PAIRS) * SESSIONS, LANES), jnp.float32)]
-    )
-    gram = times_rows(ones, crossed)
+    spare = jnp.zeros((LANES - PICKS, LANES), jnp.float32)
+    right = jnp.concatenate([rows, spare])
+    other_right = jnp.concatenate([other_rows, spare])
+    gram = times_rows(rows, right) + times_rows(other_rows, other_right)
+    crossed = [
+        jnp.sum(
+            jnp.where(lane % SESSIONS == step, gram[t * SESSIONS : (t + 1) * SESSIONS], 0.0),
+            axis=0,
+            keepdims=True,
+        )
+        for t in range(STEPS)
+    ]
+    unit = (lax.broadcasted_iota(jnp.int32, (LANES, LANES), 0) == PICKS).astype(jnp.float32)
     for q in range(out_ref.shape[0]):
         norms = []
         for h in range(2):
             at = pl.ds((2 * q + h) * LANES, LANES)
             mine, got = mine_ref[at, :], got_ref[at, :]
-            out_ref[q, pl.ds(h * PICKS, PICKS), :] = times_rows(rows, mine) + times_rows(other_rows, got)
-            norms.append(times_rows(ones, mine * mine + got * got))
-        out_ref[q, pl.ds(2 * PICKS, 8), :] = in_rows([*norms, gram[:, :LANES], gram[:, LANES:]])
+            product = times_rows(mine, right) + times_rows(got, other_right)
+            product = product + times_rows(mine * mine + got * got, unit)
+            turned = product.T
+            out_ref[q, pl.ds(h * PICKS, PICKS), :] = turned[:PICKS]
+            norms.append(turned[PICKS : PICKS + 1])
+        out_ref[q, pl.ds(2 * PICKS, 8), :] = in_rows([*norms, *crossed])
 
 
 def columns_kernel(parts_ref, out_ref):
@@ -95,10 +105,10 @@
     session = lax.broadcasted_iota(jnp.int32, (SESSIONS, LANES), 0)
     lane = lax.broadcasted_iota(jnp.int32, (SESSIONS, LANES), 1)
     gram = {}
-    for i, pair in enumerate(PAIRS):
-        row = total[2 * PICKS + 2 + i // 4 : 2 * PICKS + 3 + i // 4]
-        picked = jnp.where(lane == (i % 4) * SESSIONS + session, jnp.broadcast_to(row, session.shape), 0.0)
-        gram[pair] = jnp.sum(picked, axis=1, keepdims=True)
+    for t, u in PAIRS:
+        row = total[2 * PICKS + 2 + t : 2 * PICKS + 3 + t]
+        picked = jnp.where(lane == u * SESSIONS + session, jnp.broadcast_to(row, session.shape), 0.0)
+        gram[t, u] = jnp.sum(picked, axis=1, keepdims=True)
     factor, radius = {}, []
     for k in range(STEPS):
         left = gram[k, k]
@@ -168,6 +178,7 @@
         in_specs=[VMEM] * 4,
         out_specs=VMEM,
         cost_estimate=pl.CostEstimate(flops=2 * PICKS * half * 256, bytes_accessed=2 << 20, transcendentals=0),
+        compiler_params=PARAMS,
     )(own_rows, other_rows, mine, got)
     parts = lax.all_to_all(products, "feat_hi", 0, 0, tiled=True)
     share = pl.pallas_call(
@@ -176,6 +187,7 @@
         in_specs=[VMEM],
         out_specs=VMEM,
         cost_estimate=pl.CostEstimate(flops=1 << 20, bytes_accessed=2 << 20, transcendentals=0),
+        compiler_params=PARAMS,
     )(parts)
     spread = lax.all_to_all(share, FEAT, 0, 0, tiled=True)
     tops = jnp.max(spread[:, 2 * PICKS + 2, :], axis=0)
@@ -190,6 +202,7 @@
         in_specs=[VMEM],
         out_specs=(VMEM, VMEM),
         cost_estimate=pl.CostEstimate(flops=1 << 20, bytes_accessed=2 << 20, transcendentals=0),
+        compiler_params=PARAMS,
     )(spread)
     return (columns.transpose(1, 0, 2), gains, best)
 

time: 124 us -> 118 us (0.952)
  Pallas kernels: 9.26 us -> 3.83 us
  waiting for transfers between devices: 21.2 us -> 23.8 us
  local copies, waits for them, and re-layouts: 4.68 us -> 3.02 us
    pallas_call x1, Pallas kernels: 4.96 us -> 2.56 us  [selection(): pl.pallas_call(products_kernel, out_shape=jax.ShapeDtypeStruct((his, *pie...]
    all_to_all x2, waiting for transfers between devices: 12.5 us -> 14.5 us  [share_with(): return lax.all_to_all(copies, axes, 0, 0, tiled=True)]
    pallas_call x1, Pallas kernels: 2.11 us -> 0.21 us  [selection(): pl.pallas_call(columns_kernel, out_shape=jax.ShapeDtypeStruct((2 * his, *...]
  transfers between devices with their start and end apart: 3 -> 3, of which waited for: 3 -> 3; matrix products, arithmetic and copies ran while one was open for 1% -> 0% of each run, Pallas kernels for 2% -> 1%
where the time goes in v2:
time: 118 us; the launch traced here: 117 us
  blocking collectives  65.1 us (55%)
  waiting for transfers between devices  23.8 us (20%)
  starting transfers between devices  18.9 us (16%)
  Pallas kernels  3.83 us (3%)
  local copies, waits for them, and re-layouts  3.02 us (3%)
  matrix products  1.76 us (1%)
    all_to_all x1, blocking collectives, selection(): spread = lax.all_to_all(share, FEAT, 0, 0, tiled=True)  26 us
    all_to_all x1, blocking collectives, share_with(): return lax.all_to_all(copies, axes, 0, 0, tiled=True)  21.1 us
    all_to_all x1, blocking collectives, selection(): parts = lax.all_to_all(products, 'feat_hi', 0, 0, tiled=True)  17.9 us
    all_to_all x2, starting transfers between devices, share_with(): return lax.all_to_all(copies, axes, 0, 0, tiled=True)  15.6 us
    all_to_all x2, waiting for transfers between devices, share_with(): return lax.all_to_all(copies, axes, 0, 0, tiled=True)  14.5 us
    ppermute x1, waiting for transfers between devices, selection(): got = lax.ppermute(other, 'feat_lo', [(0, 1), (1, 0)])  9.29 us
    ppermute x1, starting transfers between devices, selection(): got = lax.ppermute(other, 'feat_lo', [(0, 1), (1, 0)])  3.26 us
    pallas_call x1, Pallas kernels, selection(): pl.pallas_call(products_kernel, out_shape=jax.ShapeDtypeStruct((his, *pie...  2.56 us
  transfers between devices with their start and end apart: 3, of which 3 were waited for; matrix products, arithmetic and copies ran while one was open for 0% of the time, Pallas kernels for 1%

profile of v2, /device:TPU:1, one launch (start us, length us, event | category | flops | bytes accessed | tf_op | source)
XLA Modules:
  0.0 117.3 jit_solution(12242613645778088411)
XLA Ops:
  0.7 0.0 copy-start.1
  0.7 0.7 copy-done.1
  1.4 0.1 eq.21
  1.4 1.8 %fusion = f32[64,128]{1,0:T(8,128)S(1)} fusion(f32[2048,128]{1,0:T(8,128)} %param.2, s32[2048]{0:T(1024)S(1)} %iota_add_fusion, s32[64]{0:T(128)S(1)} %eq.21), kind=kOutput, calls=%fused_computation | convolution fusion | flops 201457664 | bytes 1089792 | tf_op jit(solution)/shard_map/dot_general | solution.py:46
  3.2 21.1 %all_to_all.25 = f32[8,64,128]{2,1,0:T(8,128)S(1)} all-to-all(f32[8,64,128]{2,1,0:T(8,128)S(1)} %broadcast_in_dim.10), channel_id=1, replica_groups=mesh['cand_0'=4,'cand_1'=2,'blk'=8,'feat_hi'=4,'feat_lo'=2] {'blk'}, dimensions={0} | all-to-all | bytes 524288 | tf_op jit(solution)/shard_map/all_to_all | solution.py:29
  24.4 0.0 copy-start
  24.4 0.8 broadcast_in_dim.11
  25.2 7.7 %all-to-all-start.1 = ((f32[16,64,128]{2,1,0:T(8,128)}), f32[16,64,128]{2,1,0:T(8,128)S(1)}, u32[]{:S(2)}, u32[]{:S(2)}) async-start(f32[16,64,128]{2,1,0:T(8,128)} %broadcast_in_dim.11), calls=%async_computation.1 | async-start | bytes 1048576 | tf_op jit(solution)/shard_map/all_to_all | solution.py:29
  32.9 0.0 copy-done
  32.9 0.1 constant_dynamic-slice_fusion
  33.0 3.3 %collective-permute-start = (f32[1024,128]{1,0:T(8,128)S(1)}, f32[1024,128]{1,0:T(8,128)S(1)}, u32[]{:S(2)}, u32[]{:S(2)}) collective-permute-start(f32[1024,128]{1,0:T(8,128)S(1)} %get-tuple-element.7), channel_id=1, source_target_pairs={{0,1},{1,0},{2,3},{3,2},{4,5},{5,4},{6,7},{7,6},{8,9},{9,8},{10,11... | collective-permute-start | bytes 1572872 | tf_op jit(solution)/shard_map/ppermute | solution.py:170
  36.3 6.3 %all-to-all-done.1 = f32[16,64,128]{2,1,0:T(8,128)S(1)} async-done(((f32[16,64,128]{2,1,0:T(8,128)}), f32[16,64,128]{2,1,0:T(8,128)S(1)}, u32[]{:S(2)}, u32[]{:S(2)}) %all-to-all-start.1) | async-done | bytes 524320 | tf_op jit(solution)/shard_map/all_to_all | solution.py:29
  42.7 9.3 %collective-permute-done.got_ref = f32[1024,128]{1,0:T(8,128)S(1)} collective-permute-done((f32[1024,128]{1,0:T(8,128)S(1)}, f32[1024,128]{1,0:T(8,128)S(1)}, u32[]{:S(2)}, u32[]{:S(2)}) %collective-permute-start) | collective-permute-done | bytes 524320 | tf_op jit(solution)/shard_map/ppermute | solution.py:170
  52.0 2.6 %shard_map.49 = f32[4,200,128]{2,1,0:T(8,128)S(1)} custom-call(f32[96,128]{1,0:T(8,128)S(1)} %bitcast.11, f32[96,128]{1,0:T(8,128)S(1)} %bitcast.10, f32[1024,128]{1,0:T(8,128)S(1)} %get-tuple-element.8.mine_ref, f32[1024,128]{1,0:T(8,128)S(1)} %collective-permute-done.got_ref), custom_call_target="tpu_custom_call" | custom-call | flops 50331648 | bytes 2097152 | tf_op jit(solution)/shard_map/pallas_call | solution.py:175
  54.6 17.9 %all_to_all.26.parts_ref = f32[4,200,128]{2,1,0:T(8,128)S(1)} all-to-all(f32[4,200,128]{2,1,0:T(8,128)S(1)} %shard_map.49), channel_id=1, replica_groups=mesh['cand_0'=4,'cand_1'=2,'blk'=8,'feat_hi'=4,'feat_lo'=2] {'feat_hi'}, dimensions={0} | all-to-all | bytes 819200 | tf_op jit(solution)/shard_map/all_to_all | solution.py:183
  72.5 0.2 shard_map.50
  72.7 26.0 %all_to_all.27.spread_ref = f32[8,200,128]{2,1,0:T(8,128)S(1)} all-to-all(f32[8,200,128]{2,1,0:T(8,128)S(1)} %shard_map.50), channel_id=1, replica_groups=mesh['cand_0'=4,'cand_1'=2,'blk'=8,'feat_hi'=4,'feat_lo'=2] {'feat_hi','..., dimensions={0} | all-to-all | bytes 1638400 | tf_op jit(solution)/shard_map/all_to_all | solution.py:192
  98.8 0.6 broadcast_in_dim.12
  99.4 8.0 %all-to-all-start.4 = ((f32[64,1,128]{2,1,0:T(1,128)}), f32[64,1,128]{2,1,0:T(1,128)S(1)}, u32[]{:S(2)}, u32[]{:S(2)}) async-start(f32[64,1,128]{2,1,0:T(1,128)} %broadcast_in_dim.12), calls=%async_computation.4 | async-start | bytes 65536 | tf_op jit(solution)/shard_map/all_to_all | solution.py:29
  107.3 1.1 shard_map.51
  108.4 8.2 %all-to-all-done.4 = f32[64,1,128]{2,1,0:T(1,128)S(1)} async-done(((f32[64,1,128]{2,1,0:T(1,128)}), f32[64,1,128]{2,1,0:T(1,128)S(1)}, u32[]{:S(2)}, u32[]{:S(2)}) %all-to-all-start.4) | async-done | bytes 32800 | tf_op jit(solution)/shard_map/all_to_all | solution.py:29
  116.6 0.7 reshape.35
  (13 shorter events, 0.2 us)
Async XLA Ops:
  0.7 0.7 copy-start.1
  24.4 8.5 %copy-start = (f32[2048,128]{1,0:T(8,128)S(1)}, f32[2048,128]{1,0:T(8,128)}, u32[]{:S(2)}) copy-start(f32[2048,128]{1,0:T(8,128)} %param.2) | copy-start | bytes 3145732
  25.2 17.3 %all-to-all-start.1 = ((f32[16,64,128]{2,1,0:T(8,128)}), f32[16,64,128]{2,1,0:T(8,128)S(1)}, u32[]{:S(2)}, u32[]{:S(2)}) async-start(f32[16,64,128]{2,1,0:T(8,128)} %broadcast_in_dim.11), calls=%async_computation.1 | async-start | bytes 1048576 | tf_op jit(solution)/shard_map/all_to_all | solution.py:29
  33.0 19.0 %collective-permute-start = (f32[1024,128]{1,0:T(8,128)S(1)}, f32[1024,128]{1,0:T(8,128)S(1)}, u32[]{:S(2)}, u32[]{:S(2)}) collective-permute-start(f32[1024,128]{1,0:T(8,128)S(1)} %get-tuple-element.7), channel_id=1, source_target_pairs={{0,1},{1,0},{2,3},{3,2},{4,5},{5,4},{6,7},{7,6},{8,9},{9,8},{10,11... | collective-permute-start | bytes 1572872 | tf_op jit(solution)/shard_map/ppermute | solution.py:170
  99.4 17.2 %all-to-all-start.4 = ((f32[64,1,128]{2,1,0:T(1,128)}), f32[64,1,128]{2,1,0:T(1,128)S(1)}, u32[]{:S(2)}, u32[]{:S(2)}) async-start(f32[64,1,128]{2,1,0:T(1,128)} %broadcast_in_dim.12), calls=%async_computation.4 | async-start | bytes 65536 | tf_op jit(solution)/shard_map/all_to_all | solution.py:29

commit v3 on v2

--- a/solution.py
+++ b/solution.py
@@ -148,17 +148,18 @@
         out_ref[f] = whole
 
 
-def results_kernel(spread_ref, columns_ref, gains_ref):
-    his = spread_ref.shape[0] // 2
-    for f in range(2 * his):
-        for h in range(2):
-            at = pl.ds(((f % 2) * his + f // 2) * 2 * LANES + h * LANES, LANES)
-            gains = jnp.broadcast_to(spread_ref[f, pl.ds(2 * PICKS + h, 1), :], (SESSIONS, LANES))
-            for k in range(STEPS):
-                column = spread_ref[f, pl.ds(h * PICKS + k * SESSIONS, SESSIONS), :]
-                columns_ref[k, :, at] = column
-                gains = gains - column * column
-            gains_ref[:, at] = gains
+def results_kernel(side_ref, own_ref, other_ref, columns_ref, gains_ref):
+    his = own_ref.shape[0]
+    for side, ref in ((side_ref[0], own_ref), (1 - side_ref[0], other_ref)):
+        for q in range(his):
+            for h in range(2):
+                at = pl.ds(pl.multiple_of((side * his + q) * 2 * LANES + h * LANES, LANES), LANES)
+                gains = jnp.broadcast_to(ref[q, pl.ds(2 * PICKS + h, 1), :], (SESSIONS, LANES))
+                for k in range(STEPS):
+                    column = ref[q, pl.ds(h * PICKS + k * SESSIONS, SESSIONS), :]
+                    columns_ref[k, :, at] = column
+                    gains = gains - column * column
+                gains_ref[:, at] = gains
 
 
 def selection(embeddings, winners):
@@ -166,8 +167,8 @@
     his, half = lax.axis_size("feat_hi"), rows_here // 2
     side = lax.axis_index("feat_lo")
     mine = lax.dynamic_slice_in_dim(embeddings, side * half, half)
-    other = lax.dynamic_slice_in_dim(embeddings, (1 - side) * half, half)
-    got = lax.ppermute(other, "feat_lo", [(0, 1), (1, 0)])
+    away = lax.dynamic_slice_in_dim(embeddings, (1 - side) * half, half)
+    got = lax.ppermute(away, "feat_lo", [(0, 1), (1, 0)])
     rows = winner_rows(embeddings, winners)
     own_rows = jnp.where(side == 0, rows[0], rows[1])
     other_rows = jnp.where(side == 0, rows[1], rows[0])
@@ -183,15 +184,16 @@
     parts = lax.all_to_all(products, "feat_hi", 0, 0, tiled=True)
     share = pl.pallas_call(
         columns_kernel,
-        out_shape=jax.ShapeDtypeStruct((2 * his, *piece), jnp.float32),
+        out_shape=jax.ShapeDtypeStruct((his, *piece), jnp.float32),
         in_specs=[VMEM],
         out_specs=VMEM,
         cost_estimate=pl.CostEstimate(flops=1 << 20, bytes_accessed=2 << 20, transcendentals=0),
         compiler_params=PARAMS,
     )(parts)
-    spread = lax.all_to_all(share, FEAT, 0, 0, tiled=True)
-    tops = jnp.max(spread[:, 2 * PICKS + 2, :], axis=0)
-    best = share_with(tops.reshape(1, LANES), CAND_BLK).max(axis=(0, 1))
+    own = lax.all_to_all(share, "feat_hi", 0, 0, tiled=True)
+    other = lax.ppermute(own, "feat_lo", [(0, 1), (1, 0)])
+    tops = jnp.max(own[:, 2 * PICKS + 2, :], axis=0)
+    best = share_with(tops.reshape(1, LANES), (*CAND_BLK, "feat_lo")).max(axis=(0, 1))
     best = best[:PICKS].reshape(STEPS, SESSIONS).T
     columns, gains = pl.pallas_call(
         results_kernel,
@@ -199,11 +201,11 @@
             jax.ShapeDtypeStruct((STEPS, SESSIONS, rows_here), jnp.float32),
             jax.ShapeDtypeStruct((SESSIONS, rows_here), jnp.float32),
         ),
-        in_specs=[VMEM],
+        in_specs=[pl.BlockSpec(memory_space=pltpu.SMEM), VMEM, VMEM],
         out_specs=(VMEM, VMEM),
         cost_estimate=pl.CostEstimate(flops=1 << 20, bytes_accessed=2 << 20, transcendentals=0),
         compiler_params=PARAMS,
-    )(spread)
+    )(side.reshape(1), own, other)
     return (columns.transpose(1, 0, 2), gains, best)
 
 

time: 118 us -> 113 us (0.958)
  blocking collectives: 65.1 us -> 75.1 us
  waiting for transfers between devices: 23.8 us -> 15.6 us
  starting transfers between devices: 18.9 us -> 12.8 us
    all_to_all x1 -> x2, blocking collectives: 21.1 us -> 42 us  [share_with(): return lax.all_to_all(copies, axes, 0, 0, tiled=True)]
    all_to_all x1, blocking collectives: 26 us -> 15.2 us  [selection(): own = lax.all_to_all(share, 'feat_hi', 0, 0, tiled=True)]
    all_to_all x2 -> x1, waiting for transfers between devices: 14.5 us -> 6.27 us  [share_with(): return lax.all_to_all(copies, axes, 0, 0, tiled=True)]
    all_to_all x2 -> x1, starting transfers between devices: 15.6 us -> 7.66 us  [share_with(): return lax.all_to_all(copies, axes, 0, 0, tiled=True)]
    ppermute x1 -> x2, starting transfers between devices: 3.26 us -> 5.17 us  [the longest x1 3.26 us: selection(): got = lax.ppermute(away, 'feat_lo', [(0, 1), (1, 0)])]
    ppermute x1 -> x2, waiting for transfers between devices: 9.29 us -> 9.29 us  [the longest x1 9.29 us: selection(): got = lax.ppermute(away, 'feat_lo', [(0, 1), (1, 0)])]
  transfers between devices with their start and end apart: 3 -> 3, of which waited for: 3 -> 2; matrix products, arithmetic and copies ran while one was open for 0% -> 1% of each run, Pallas kernels for 1% -> 0%
where the time goes in v3:
time: 113 us; the launch traced here: 112 us
  blocking collectives  75.1 us (66%)
  waiting for transfers between devices  15.6 us (14%)
  starting transfers between devices  12.8 us (11%)
  Pallas kernels  3.83 us (3%)
  local copies, waits for them, and re-layouts  2.44 us (2%)
  matrix products  1.76 us (2%)
    all_to_all x2, blocking collectives, share_with(): return lax.all_to_all(copies, axes, 0, 0, tiled=True)  42 us
    all_to_all x1, blocking collectives, selection(): parts = lax.all_to_all(products, 'feat_hi', 0, 0, tiled=True)  17.9 us
    all_to_all x1, blocking collectives, selection(): own = lax.all_to_all(share, 'feat_hi', 0, 0, tiled=True)  15.2 us
    ppermute x1, waiting for transfers between devices, selection(): got = lax.ppermute(away, 'feat_lo', [(0, 1), (1, 0)])  9.29 us
    all_to_all x1, starting transfers between devices, share_with(): return lax.all_to_all(copies, axes, 0, 0, tiled=True)  7.66 us
    all_to_all x1, waiting for transfers between devices, share_with(): return lax.all_to_all(copies, axes, 0, 0, tiled=True)  6.27 us
    ppermute x1, starting transfers between devices, selection(): got = lax.ppermute(away, 'feat_lo', [(0, 1), (1, 0)])  3.26 us
    pallas_call x1, Pallas kernels, selection(): pl.pallas_call(products_kernel, out_shape=jax.ShapeDtypeStruct((his, *pie...  2.56 us
  transfers between devices with their start and end apart: 3, of which 2 were waited for; matrix products, arithmetic and copies ran while one was open for 1% of the time, Pallas kernels for 0%

profile of v3, /device:TPU:1, one launch (start us, length us, event | category | flops | bytes accessed | tf_op | source)
XLA Modules:
  0.0 112.5 jit_solution(6732092615663717269)
XLA Ops:
  0.7 0.0 copy-start.1
  0.7 0.7 copy-done.1
  1.4 0.1 eq.21
  1.4 1.8 %fusion = f32[64,128]{1,0:T(8,128)S(1)} fusion(f32[2048,128]{1,0:T(8,128)} %param.2, s32[2048]{0:T(1024)S(1)} %iota_add_fusion, s32[64]{0:T(128)S(1)} %eq.21), kind=kOutput, calls=%fused_computation | convolution fusion | flops 201457664 | bytes 1089792 | tf_op jit(solution)/shard_map/dot_general | solution.py:46
  3.2 21.1 %all_to_all.25 = f32[8,64,128]{2,1,0:T(8,128)S(1)} all-to-all(f32[8,64,128]{2,1,0:T(8,128)S(1)} %broadcast_in_dim.10), channel_id=1, replica_groups=mesh['cand_0'=4,'cand_1'=2,'blk'=8,'feat_hi'=4,'feat_lo'=2] {'blk'}, dimensions={0} | all-to-all | bytes 524288 | tf_op jit(solution)/shard_map/all_to_all | solution.py:29
  24.4 0.0 copy-start
  24.4 0.8 broadcast_in_dim.11
  25.2 7.7 %all-to-all-start.1 = ((f32[16,64,128]{2,1,0:T(8,128)}), f32[16,64,128]{2,1,0:T(8,128)S(1)}, u32[]{:S(2)}, u32[]{:S(2)}) async-start(f32[16,64,128]{2,1,0:T(8,128)} %broadcast_in_dim.11), calls=%async_computation.1 | async-start | bytes 1048576 | tf_op jit(solution)/shard_map/all_to_all | solution.py:29
  32.9 0.0 copy-done
  32.9 0.1 constant_dynamic-slice_fusion
  33.0 3.3 %collective-permute-start = (f32[1024,128]{1,0:T(8,128)S(1)}, f32[1024,128]{1,0:T(8,128)S(1)}, u32[]{:S(2)}, u32[]{:S(2)}) collective-permute-start(f32[1024,128]{1,0:T(8,128)S(1)} %get-tuple-element.7), channel_id=1, source_target_pairs={{0,1},{1,0},{2,3},{3,2},{4,5},{5,4},{6,7},{7,6},{8,9},{9,8},{10,11... | collective-permute-start | bytes 1572872 | tf_op jit(solution)/shard_map/ppermute | solution.py:171
  36.3 6.3 %all-to-all-done.1 = f32[16,64,128]{2,1,0:T(8,128)S(1)} async-done(((f32[16,64,128]{2,1,0:T(8,128)}), f32[16,64,128]{2,1,0:T(8,128)S(1)}, u32[]{:S(2)}, u32[]{:S(2)}) %all-to-all-start.1) | async-done | bytes 524320 | tf_op jit(solution)/shard_map/all_to_all | solution.py:29
  42.7 9.3 %collective-permute-done.got_ref = f32[1024,128]{1,0:T(8,128)S(1)} collective-permute-done((f32[1024,128]{1,0:T(8,128)S(1)}, f32[1024,128]{1,0:T(8,128)S(1)}, u32[]{:S(2)}, u32[]{:S(2)}) %collective-permute-start) | collective-permute-done | bytes 524320 | tf_op jit(solution)/shard_map/ppermute | solution.py:171
  52.0 2.6 %shard_map.49 = f32[4,200,128]{2,1,0:T(8,128)S(1)} custom-call(f32[96,128]{1,0:T(8,128)S(1)} %bitcast.12, f32[96,128]{1,0:T(8,128)S(1)} %bitcast.11, f32[1024,128]{1,0:T(8,128)S(1)} %get-tuple-element.8.mine_ref, f32[1024,128]{1,0:T(8,128)S(1)} %collective-permute-done.got_ref), custom_call_target="tpu_custom_call" | custom-call | flops 50331648 | bytes 2097152 | tf_op jit(solution)/shard_map/pallas_call | solution.py:176
  54.6 17.9 %all_to_all.26.parts_ref = f32[4,200,128]{2,1,0:T(8,128)S(1)} all-to-all(f32[4,200,128]{2,1,0:T(8,128)S(1)} %shard_map.49), channel_id=1, replica_groups=mesh['cand_0'=4,'cand_1'=2,'blk'=8,'feat_hi'=4,'feat_lo'=2] {'feat_hi'}, dimensions={0} | all-to-all | bytes 819200 | tf_op jit(solution)/shard_map/all_to_all | solution.py:184
  72.5 0.2 shard_map.50
  72.7 15.2 %all_to_all.27.own_ref = f32[4,200,128]{2,1,0:T(8,128)S(1)} all-to-all(f32[4,200,128]{2,1,0:T(8,128)S(1)} %shard_map.50), channel_id=1, replica_groups=mesh['cand_0'=4,'cand_1'=2,'blk'=8,'feat_hi'=4,'feat_lo'=2] {'feat_hi'}, dimensions={0} | all-to-all | bytes 819200 | tf_op jit(solution)/shard_map/all_to_all | solution.py:193
  87.9 1.9 %collective-permute-start.1 = (f32[4,200,128]{2,1,0:T(8,128)S(1)}, f32[4,200,128]{2,1,0:T(8,128)S(1)}, u32[]{:S(2)}, u32[]{:S(2)}) collective-permute-start(f32[4,200,128]{2,1,0:T(8,128)S(1)} %all_to_all.27.own_ref), channel_id=1, source_target_pairs={{0,1},{1,0},{2,3},{3,2},{4,5},{5,4},{6,7},{7,6},{8,9},{9,8},{10,11... | collective-permute-start | bytes 1228808 | tf_op jit(solution)/shard_map/ppermute | solution.py:194
  89.9 20.8 %all_to_all.28 = f32[128,1,128]{2,1,0:T(1,128)S(1)} all-to-all(f32[128,1,128]{2,1,0:T(1,128)S(1)} %broadcast_in_dim.12), channel_id=1, replica_groups=mesh['cand_0'=4,'cand_1'=2,'blk'=8,'feat_hi'=4,'feat_lo'=2] {'cand_0','c..., dimensions={0} | all-to-all | bytes 131072 | tf_op jit(solution)/shard_map/all_to_all | solution.py:29
  110.8 0.7 reshape.39
  111.4 0.0 collective-permute-done.1.other_ref
  111.4 1.1 shard_map.51
  (14 shorter events, 0.3 us)
Async XLA Ops:
  0.7 0.7 copy-start.1
  24.4 8.5 %copy-start = (f32[2048,128]{1,0:T(8,128)S(1)}, f32[2048,128]{1,0:T(8,128)}, u32[]{:S(2)}) copy-start(f32[2048,128]{1,0:T(8,128)} %param.2) | copy-start | bytes 3145732
  25.2 17.3 %all-to-all-start.1 = ((f32[16,64,128]{2,1,0:T(8,128)}), f32[16,64,128]{2,1,0:T(8,128)S(1)}, u32[]{:S(2)}, u32[]{:S(2)}) async-start(f32[16,64,128]{2,1,0:T(8,128)} %broadcast_in_dim.11), calls=%async_computation.1 | async-start | bytes 1048576 | tf_op jit(solution)/shard_map/all_to_all | solution.py:29
  33.0 19.0 %collective-permute-start = (f32[1024,128]{1,0:T(8,128)S(1)}, f32[1024,128]{1,0:T(8,128)S(1)}, u32[]{:S(2)}, u32[]{:S(2)}) collective-permute-start(f32[1024,128]{1,0:T(8,128)S(1)} %get-tuple-element.7), channel_id=1, source_target_pairs={{0,1},{1,0},{2,3},{3,2},{4,5},{5,4},{6,7},{7,6},{8,9},{9,8},{10,11... | collective-permute-start | bytes 1572872 | tf_op jit(solution)/shard_map/ppermute | solution.py:171
  87.9 23.5 %collective-permute-start.1 = (f32[4,200,128]{2,1,0:T(8,128)S(1)}, f32[4,200,128]{2,1,0:T(8,128)S(1)}, u32[]{:S(2)}, u32[]{:S(2)}) collective-permute-start(f32[4,200,128]{2,1,0:T(8,128)S(1)} %all_to_all.27.own_ref), channel_id=1, source_target_pairs={{0,1},{1,0},{2,3},{3,2},{4,5},{5,4},{6,7},{7,6},{8,9},{9,8},{10,11... | collective-permute-start | bytes 1228808 | tf_op jit(solution)/shard_map/ppermute | solution.py:194

commit v4 on v3

--- a/solution.py
+++ b/solution.py
@@ -1,3 +1,5 @@
+import functools
+
 import jax
 import jax.numpy as jnp
 from jax import lax
@@ -20,6 +22,8 @@
 EXACT = lax.Precision.HIGHEST
 PAIRS = [(t, u) for t in range(STEPS) for u in range(t, STEPS)]
 VMEM = pl.BlockSpec(memory_space=pltpu.VMEM)
+HBM = pl.BlockSpec(memory_space=pl.ANY)
+SMEM = pl.BlockSpec(memory_space=pltpu.SMEM)
 PARAMS = pltpu.CompilerParams(vmem_limit_bytes=12 << 20)
 
 
@@ -33,18 +37,49 @@
     return min(group * (CANDS // groups) // (CANDS // STEPS), STEPS - 2)
 
 
+def picks_kernel(turn, winners_hbm, embeddings_hbm, out_ref, winners_ref, embeddings_ref, sems):
+    fetch_rows = pltpu.make_async_copy(embeddings_hbm, embeddings_ref, sems.at[0])
+    fetch_winners = pltpu.make_async_copy(winners_hbm, winners_ref, sems.at[1])
+    fetch_rows.start()
+    fetch_winners.start()
+    fetch_winners.wait()
+    fetch_rows.wait()
+    rows_here = embeddings_ref.shape[0]
+    first = (lax.axis_index(CAND) >= turn).astype(jnp.int32)
+    offset = lax.axis_index(CAND_BLK) * rows_here
+    at = lax.broadcasted_iota(jnp.int32, (8, LANES), 0)
+    for start in range(0, 2 * SESSIONS, 8):
+        tile = jnp.zeros((8, LANES), jnp.float32)
+        for row in range(8):
+            step, session = divmod(start + row, SESSIONS)
+            here = winners_ref[first + step, session] - offset
+            held = jnp.logical_and(here >= 0, here < rows_here)
+            values = embeddings_ref[pl.ds(jnp.clip(here, 0, rows_here - 1), 1), :]
+            wanted = jnp.logical_and(at == row, held)
+            tile = jnp.where(wanted, jnp.broadcast_to(values, (8, LANES)), tile)
+        for copy in range(out_ref.shape[0]):
+            out_ref[copy, pl.ds(start, 8), :] = tile
+
+
 def winner_rows(embeddings, winners):
     rows_here, width = embeddings.shape
     groups = lax.axis_size(CAND)
     turn = [first_step(g, groups) for g in range(groups)].index(1)
-    late = lax.axis_index(CAND) >= turn
-    offset = lax.axis_index(CAND_BLK) * rows_here
-    by_step = winners.T
-    chosen = jnp.where(late, by_step[1:], by_step[:2]).reshape(2 * SESSIONS)
-    positions = offset + jnp.arange(rows_here, dtype=jnp.int32)
-    onehot = (positions[None, :] == chosen[:, None]).astype(jnp.float32)
-    part = jnp.dot(onehot, embeddings, precision=EXACT, preferred_element_type=jnp.float32)
-    group_rows = jnp.sum(share_with(part, "blk"), axis=0)
+    blks = lax.axis_size("blk")
+    part = pl.pallas_call(
+        functools.partial(picks_kernel, turn),
+        out_shape=jax.ShapeDtypeStruct((blks, 2 * SESSIONS, width), jnp.float32),
+        in_specs=[HBM, HBM],
+        out_specs=VMEM,
+        scratch_shapes=[
+            pltpu.SMEM((STEPS, SESSIONS), jnp.int32),
+            pltpu.VMEM((rows_here, width), jnp.float32),
+            pltpu.SemaphoreType.DMA((2,)),
+        ],
+        cost_estimate=pl.CostEstimate(flops=1 << 20, bytes_accessed=1 << 20, transcendentals=0),
+    )(winners.T, embeddings)
+    part = lax.all_to_all(part, "blk", 0, 0, tiled=True)
+    group_rows = jnp.sum(part, axis=0)
     spread = share_with(group_rows, (*CAND, "feat_lo"))
     spread = spread.reshape(groups, 2, 2, SESSIONS, width)
     low = jnp.sum(spread[:turn], axis=0)
@@ -67,31 +102,30 @@
     return tile
 
 
-def products_kernel(rows_ref, other_rows_ref, mine_ref, got_ref, out_ref):
-    step = lax.broadcasted_iota(jnp.int32, (SESSIONS, LANES), 0)
+def products_kernel(side_ref, rows_ref, mine_ref, got_ref, out_ref):
+    session = lax.broadcasted_iota(jnp.int32, (SESSIONS, LANES), 0)
     lane = lax.broadcasted_iota(jnp.int32, (SESSIONS, LANES), 1)
-    rows, other_rows = rows_ref[...], other_rows_ref[...]
-    spare = jnp.zeros((LANES - PICKS, LANES), jnp.float32)
-    right = jnp.concatenate([rows, spare])
-    other_right = jnp.concatenate([other_rows, spare])
-    gram = times_rows(rows, right) + times_rows(other_rows, other_right)
+    rows = jnp.concatenate([rows_ref[side_ref[0]], rows_ref[1 - side_ref[0]]], axis=1)
+    right = jnp.concatenate([rows, jnp.zeros((LANES - PICKS, 2 * LANES), jnp.float32)])
+    gram = times_rows(rows, right)
     crossed = [
         jnp.sum(
-            jnp.where(lane % SESSIONS == step, gram[t * SESSIONS : (t + 1) * SESSIONS], 0.0),
+            jnp.where(lane % SESSIONS == session, gram[t * SESSIONS : (t + 1) * SESSIONS], 0.0),
             axis=0,
             keepdims=True,
         )
         for t in range(STEPS)
     ]
-    unit = (lax.broadcasted_iota(jnp.int32, (LANES, LANES), 0) == PICKS).astype(jnp.float32)
+    norm_lane = lax.broadcasted_iota(jnp.int32, (2 * LANES, LANES), 1) == PICKS
     for q in range(out_ref.shape[0]):
+        at = pl.ds(q * 2 * LANES, 2 * LANES)
+        mine, got = mine_ref[at, :], got_ref[at, :]
+        product = times_rows(jnp.concatenate([mine, got], axis=1), right)
+        norm = jnp.sum(mine * mine + got * got, axis=1, keepdims=True)
+        product = jnp.where(norm_lane, norm, product)
         norms = []
         for h in range(2):
-            at = pl.ds((2 * q + h) * LANES, LANES)
-            mine, got = mine_ref[at, :], got_ref[at, :]
-            product = times_rows(mine, right) + times_rows(got, other_right)
-            product = product + times_rows(mine * mine + got * got, unit)
-            turned = product.T
+            turned = product[h * LANES : (h + 1) * LANES].T
             out_ref[q, pl.ds(h * PICKS, PICKS), :] = turned[:PICKS]
             norms.append(turned[PICKS : PICKS + 1])
         out_ref[q, pl.ds(2 * PICKS, 8), :] = in_rows([*norms, *crossed])
@@ -170,17 +204,15 @@
     away = lax.dynamic_slice_in_dim(embeddings, (1 - side) * half, half)
     got = lax.ppermute(away, "feat_lo", [(0, 1), (1, 0)])
     rows = winner_rows(embeddings, winners)
-    own_rows = jnp.where(side == 0, rows[0], rows[1])
-    other_rows = jnp.where(side == 0, rows[1], rows[0])
     piece = (2 * PICKS + 8, LANES)
     products = pl.pallas_call(
         products_kernel,
         out_shape=jax.ShapeDtypeStruct((his, *piece), jnp.float32),
-        in_specs=[VMEM] * 4,
+        in_specs=[SMEM, VMEM, VMEM, VMEM],
         out_specs=VMEM,
         cost_estimate=pl.CostEstimate(flops=2 * PICKS * half * 256, bytes_accessed=2 << 20, transcendentals=0),
         compiler_params=PARAMS,
-    )(own_rows, other_rows, mine, got)
+    )(side.reshape(1), rows, mine, got)
     parts = lax.all_to_all(products, "feat_hi", 0, 0, tiled=True)
     share = pl.pallas_call(
         columns_kernel,
@@ -201,7 +233,7 @@
             jax.ShapeDtypeStruct((STEPS, SESSIONS, rows_here), jnp.float32),
             jax.ShapeDtypeStruct((SESSIONS, rows_here), jnp.float32),
         ),
-        in_specs=[pl.BlockSpec(memory_space=pltpu.SMEM), VMEM, VMEM],
+        in_specs=[SMEM, VMEM, VMEM],
         out_specs=(VMEM, VMEM),
         cost_estimate=pl.CostEstimate(flops=1 << 20, bytes_accessed=2 << 20, transcendentals=0),
         compiler_params=PARAMS,

time: 113 us -> 111 us (0.982)
  matrix products: 1.76 us -> 0 us
    all_to_all x0 -> x1, blocking collectives: none -> 21.4 us  [winner_rows(): part = lax.all_to_all(part, 'blk', 0, 0, tiled=True)]
    all_to_all x2 -> x1, blocking collectives: 42 us -> 20.8 us  [share_with(): return lax.all_to_all(copies, axes, 0, 0, tiled=True)]
    pallas_call x0 -> x1, Pallas kernels: none -> 2.17 us  [winner_rows(): pl.pallas_call(functools.partial(picks_kernel, turn), out_shape=jax.Shape...]
    dot_general x1 -> x0, matrix products: 1.76 us -> none  [winner_rows(): jnp.dot(onehot, embeddings, precision=EXACT, preferred_element_type=jnp.f...]
    pallas_call x1, Pallas kernels: 2.56 us -> 1.16 us  [selection(): pl.pallas_call(products_kernel, out_shape=jax.ShapeDtypeStruct((his, *pie...]
where the time goes in v4:
time: 111 us
  blocking collectives  75.3 us (68%)
  waiting for transfers between devices  15.6 us (14%)
  starting transfers between devices  12.8 us (12%)
  Pallas kernels  4.59 us (4%)
  local copies, waits for them, and re-layouts  1.66 us (1%)
    all_to_all x1, blocking collectives, winner_rows(): part = lax.all_to_all(part, 'blk', 0, 0, tiled=True)  21.4 us
    all_to_all x1, blocking collectives, share_with(): return lax.all_to_all(copies, axes, 0, 0, tiled=True)  20.8 us
    all_to_all x1, blocking collectives, selection(): parts = lax.all_to_all(products, 'feat_hi', 0, 0, tiled=True)  18 us
    all_to_all x1, blocking collectives, selection(): own = lax.all_to_all(share, 'feat_hi', 0, 0, tiled=True)  15.2 us
    ppermute x1, waiting for transfers between devices, selection(): got = lax.ppermute(away, 'feat_lo', [(0, 1), (1, 0)])  9.31 us
    all_to_all x1, starting transfers between devices, share_with(): return lax.all_to_all(copies, axes, 0, 0, tiled=True)  7.66 us
    all_to_all x1, waiting for transfers between devices, share_with(): return lax.all_to_all(copies, axes, 0, 0, tiled=True)  6.27 us
    ppermute x1, starting transfers between devices, selection(): got = lax.ppermute(away, 'feat_lo', [(0, 1), (1, 0)])  3.26 us
  transfers between devices with their start and end apart: 3, of which 2 were waited for; matrix products, arithmetic and copies ran while one was open for 1% of the time, Pallas kernels for 0%

profile of v4, /device:TPU:1, one launch (start us, length us, event | category | flops | bytes accessed | tf_op | source)
XLA Modules:
  0.0 110.9 jit_solution(5560987116120342160)
XLA Ops:
  0.6 2.2 %shard_map.49 = f32[8,64,128]{2,1,0:T(8,128)} custom-call(s32[3,32]{1,0:T(4,128)} %bitcast.13, f32[2048,128]{1,0:T(8,128)} %embeddings_hbm.1), custom_call_target="tpu_custom_call" | custom-call | flops 1048576 | bytes 1048576 | tf_op jit(solution)/shard_map/pallas_call | solution.py:69
  2.8 21.4 %all_to_all.25 = f32[8,64,128]{2,1,0:T(8,128)S(1)} all-to-all(f32[8,64,128]{2,1,0:T(8,128)} %shard_map.49), channel_id=1, replica_groups=mesh['cand_0'=4,'cand_1'=2,'blk'=8,'feat_hi'=4,'feat_lo'=2] {'blk'}, dimensions={0} | all-to-all | bytes 524288 | tf_op jit(solution)/shard_map/all_to_all | solution.py:81
  24.2 0.0 copy-start
  24.2 0.8 broadcast_in_dim.6
  25.0 7.7 %all-to-all-start.1 = ((f32[16,64,128]{2,1,0:T(8,128)}), f32[16,64,128]{2,1,0:T(8,128)S(1)}, u32[]{:S(2)}, u32[]{:S(2)}) async-start(f32[16,64,128]{2,1,0:T(8,128)} %broadcast_in_dim.6), calls=%async_computation.1 | async-start | bytes 1048576 | tf_op jit(solution)/shard_map/all_to_all | solution.py:33
  32.7 0.0 copy-done
  32.7 0.1 constant_dynamic-slice_fusion
  32.8 3.3 %collective-permute-start = (f32[1024,128]{1,0:T(8,128)S(1)}, f32[1024,128]{1,0:T(8,128)S(1)}, u32[]{:S(2)}, u32[]{:S(2)}) collective-permute-start(f32[1024,128]{1,0:T(8,128)S(1)} %get-tuple-element.7), channel_id=1, source_target_pairs={{0,1},{1,0},{2,3},{3,2},{4,5},{5,4},{6,7},{7,6},{8,9},{9,8},{10,11... | collective-permute-start | bytes 1572872 | tf_op jit(solution)/shard_map/ppermute | solution.py:205
  36.0 6.3 %all-to-all-done.1 = f32[16,64,128]{2,1,0:T(8,128)S(1)} async-done(((f32[16,64,128]{2,1,0:T(8,128)}), f32[16,64,128]{2,1,0:T(8,128)S(1)}, u32[]{:S(2)}, u32[]{:S(2)}) %all-to-all-start.1) | async-done | bytes 524320 | tf_op jit(solution)/shard_map/all_to_all | solution.py:33
  42.5 9.3 %collective-permute-done.got_ref = f32[1024,128]{1,0:T(8,128)S(1)} collective-permute-done((f32[1024,128]{1,0:T(8,128)S(1)}, f32[1024,128]{1,0:T(8,128)S(1)}, u32[]{:S(2)}, u32[]{:S(2)}) %collective-permute-start) | collective-permute-done | bytes 524320 | tf_op jit(solution)/shard_map/ppermute | solution.py:205
  51.8 1.2 %shard_map.50 = f32[4,200,128]{2,1,0:T(8,128)S(1)} custom-call(s32[1]{0:T(128)} %bitcast.side_ref, f32[2,96,128]{2,1,0:T(8,128)S(1)} %bitcast.9, f32[1024,128]{1,0:T(8,128)S(1)} %get-tuple-element.8.mine_ref, f32[1024,128]{1,0:T(8,128)S(1)} %collective-permute-done.got_ref), custom_call_target="tpu_custom_call" | custom-call | flops 50331648 | bytes 2097152 | tf_op jit(solution)/shard_map/pallas_call | solution.py:208
  52.9 18.0 %all_to_all.26.parts_ref = f32[4,200,128]{2,1,0:T(8,128)S(1)} all-to-all(f32[4,200,128]{2,1,0:T(8,128)S(1)} %shard_map.50), channel_id=1, replica_groups=mesh['cand_0'=4,'cand_1'=2,'blk'=8,'feat_hi'=4,'feat_lo'=2] {'feat_hi'}, dimensions={0} | all-to-all | bytes 819200 | tf_op jit(solution)/shard_map/all_to_all | solution.py:216
  70.9 0.2 shard_map.51
  71.1 15.2 %all_to_all.27.own_ref = f32[4,200,128]{2,1,0:T(8,128)S(1)} all-to-all(f32[4,200,128]{2,1,0:T(8,128)S(1)} %shard_map.51), channel_id=1, replica_groups=mesh['cand_0'=4,'cand_1'=2,'blk'=8,'feat_hi'=4,'feat_lo'=2] {'feat_hi'}, dimensions={0} | all-to-all | bytes 819200 | tf_op jit(solution)/shard_map/all_to_all | solution.py:225
  86.3 1.9 %collective-permute-start.1 = (f32[4,200,128]{2,1,0:T(8,128)S(1)}, f32[4,200,128]{2,1,0:T(8,128)S(1)}, u32[]{:S(2)}, u32[]{:S(2)}) collective-permute-start(f32[4,200,128]{2,1,0:T(8,128)S(1)} %all_to_all.27.own_ref), channel_id=1, source_target_pairs={{0,1},{1,0},{2,3},{3,2},{4,5},{5,4},{6,7},{7,6},{8,9},{9,8},{10,11... | collective-permute-start | bytes 1228808 | tf_op jit(solution)/shard_map/ppermute | solution.py:226
  88.3 20.8 %all_to_all.28 = f32[128,1,128]{2,1,0:T(1,128)S(1)} all-to-all(f32[128,1,128]{2,1,0:T(1,128)S(1)} %broadcast_in_dim.7), channel_id=1, replica_groups=mesh['cand_0'=4,'cand_1'=2,'blk'=8,'feat_hi'=4,'feat_lo'=2] {'cand_0','c..., dimensions={0} | all-to-all | bytes 131072 | tf_op jit(solution)/shard_map/all_to_all | solution.py:33
  109.1 0.7 reshape.30
  109.8 0.0 collective-permute-done.1.other_ref
  109.8 1.1 shard_map.52
  (10 shorter events, 0.2 us)
Async XLA Ops:
  24.2 8.5 %copy-start = (f32[2048,128]{1,0:T(8,128)S(1)}, f32[2048,128]{1,0:T(8,128)}, u32[]{:S(2)}) copy-start(f32[2048,128]{1,0:T(8,128)} %embeddings_hbm.1) | copy-start | bytes 3145732
  25.0 17.3 %all-to-all-start.1 = ((f32[16,64,128]{2,1,0:T(8,128)}), f32[16,64,128]{2,1,0:T(8,128)S(1)}, u32[]{:S(2)}, u32[]{:S(2)}) async-start(f32[16,64,128]{2,1,0:T(8,128)} %broadcast_in_dim.6), calls=%async_computation.1 | async-start | bytes 1048576 | tf_op jit(solution)/shard_map/all_to_all | solution.py:33
  32.8 19.0 %collective-permute-start = (f32[1024,128]{1,0:T(8,128)S(1)}, f32[1024,128]{1,0:T(8,128)S(1)}, u32[]{:S(2)}, u32[]{:S(2)}) collective-permute-start(f32[1024,128]{1,0:T(8,128)S(1)} %get-tuple-element.7), channel_id=1, source_target_pairs={{0,1},{1,0},{2,3},{3,2},{4,5},{5,4},{6,7},{7,6},{8,9},{9,8},{10,11... | collective-permute-start | bytes 1572872 | tf_op jit(solution)/shard_map/ppermute | solution.py:205
  86.3 23.5 %collective-permute-start.1 = (f32[4,200,128]{2,1,0:T(8,128)S(1)}, f32[4,200,128]{2,1,0:T(8,128)S(1)}, u32[]{:S(2)}, u32[]{:S(2)}) collective-permute-start(f32[4,200,128]{2,1,0:T(8,128)S(1)} %all_to_all.27.own_ref), channel_id=1, source_target_pairs={{0,1},{1,0},{2,3},{3,2},{4,5},{5,4},{6,7},{7,6},{8,9},{9,8},{10,11... | collective-permute-start | bytes 1228808 | tf_op jit(solution)/shard_map/ppermute | solution.py:226

commit v5 on v4

--- a/solution.py
+++ b/solution.py
@@ -45,30 +45,31 @@
     fetch_winners.wait()
     fetch_rows.wait()
     rows_here = embeddings_ref.shape[0]
-    first = (lax.axis_index(CAND) >= turn).astype(jnp.int32)
+    first = (lax.axis_index("cand_0") >= turn).astype(jnp.int32)
     offset = lax.axis_index(CAND_BLK) * rows_here
     at = lax.broadcasted_iota(jnp.int32, (8, LANES), 0)
-    for start in range(0, 2 * SESSIONS, 8):
-        tile = jnp.zeros((8, LANES), jnp.float32)
-        for row in range(8):
-            step, session = divmod(start + row, SESSIONS)
-            here = winners_ref[first + step, session] - offset
-            held = jnp.logical_and(here >= 0, here < rows_here)
-            values = embeddings_ref[pl.ds(jnp.clip(here, 0, rows_here - 1), 1), :]
-            wanted = jnp.logical_and(at == row, held)
-            tile = jnp.where(wanted, jnp.broadcast_to(values, (8, LANES)), tile)
-        for copy in range(out_ref.shape[0]):
-            out_ref[copy, pl.ds(start, 8), :] = tile
+    blks = out_ref.shape[0] // 2
+    for step in range(2):
+        for start in range(0, SESSIONS, 8):
+            tile = jnp.zeros((8, LANES), jnp.float32)
+            for row in range(8):
+                here = winners_ref[first + step, start + row] - offset
+                held = jnp.logical_and(here >= 0, here < rows_here)
+                values = embeddings_ref[pl.ds(jnp.clip(here, 0, rows_here - 1), 1), :]
+                wanted = jnp.logical_and(at == row, held)
+                tile = jnp.where(wanted, jnp.broadcast_to(values, (8, LANES)), tile)
+            for copy in range(blks):
+                out_ref[step * blks + copy, pl.ds(start, 8), :] = tile
 
 
 def winner_rows(embeddings, winners):
     rows_here, width = embeddings.shape
-    groups = lax.axis_size(CAND)
+    groups = lax.axis_size("cand_0")
     turn = [first_step(g, groups) for g in range(groups)].index(1)
     blks = lax.axis_size("blk")
     part = pl.pallas_call(
         functools.partial(picks_kernel, turn),
-        out_shape=jax.ShapeDtypeStruct((blks, 2 * SESSIONS, width), jnp.float32),
+        out_shape=jax.ShapeDtypeStruct((2 * blks, SESSIONS, width), jnp.float32),
         in_specs=[HBM, HBM],
         out_specs=VMEM,
         scratch_shapes=[
@@ -78,13 +79,13 @@
         ],
         cost_estimate=pl.CostEstimate(flops=1 << 20, bytes_accessed=1 << 20, transcendentals=0),
     )(winners.T, embeddings)
-    part = lax.all_to_all(part, "blk", 0, 0, tiled=True)
+    part = lax.all_to_all(part, ("cand_1", "blk"), 0, 0, tiled=True)
     group_rows = jnp.sum(part, axis=0)
     spread = share_with(group_rows, (*CAND, "feat_lo"))
     spread = spread.reshape(groups, 2, 2, SESSIONS, width)
     low = jnp.sum(spread[:turn], axis=0)
     high = jnp.sum(spread[turn:], axis=0)
-    rows = jnp.stack([low[:, 0], low[:, 1] + high[:, 0], high[:, 1]], axis=1)
+    rows = jnp.stack([low[0], low[1] + high[0], high[1]], axis=1)
     return rows.reshape(2, PICKS, width)
 
 

time: 111 us -> 109 us (0.982)
  waiting for transfers between devices: 15.6 us -> 12.8 us
  blocking collectives: 75.3 us -> 77.7 us
  starting transfers between devices: 12.8 us -> 11.3 us
    all_to_all x1, waiting for transfers between devices: 6.27 us -> 3.88 us  [share_with(): return lax.all_to_all(copies, axes, 0, 0, tiled=True)]
    all_to_all x1, blocking collectives: 20.8 us -> 22.4 us  [share_with(): return lax.all_to_all(copies, axes, 0, 0, tiled=True)]
    all_to_all x1, starting transfers between devices: 7.66 us -> 6.15 us  [share_with(): return lax.all_to_all(copies, axes, 0, 0, tiled=True)]
where the time goes in v5:
time: 109 us
  blocking collectives  77.7 us (71%)
  waiting for transfers between devices  12.8 us (12%)
  starting transfers between devices  11.3 us (10%)
  Pallas kernels  4.59 us (4%)
  local copies, waits for them, and re-layouts  1.54 us (1%)
    all_to_all x1, blocking collectives, share_with(): return lax.all_to_all(copies, axes, 0, 0, tiled=True)  22.4 us
    all_to_all x1, blocking collectives, winner_rows(): part = lax.all_to_all(part, ('cand_1', 'blk'), 0, 0, tiled=True)  21.6 us
    all_to_all x1, blocking collectives, selection(): parts = lax.all_to_all(products, 'feat_hi', 0, 0, tiled=True)  17.8 us
    all_to_all x1, blocking collectives, selection(): own = lax.all_to_all(share, 'feat_hi', 0, 0, tiled=True)  15.9 us
    ppermute x1, waiting for transfers between devices, selection(): got = lax.ppermute(away, 'feat_lo', [(0, 1), (1, 0)])  8.91 us
    all_to_all x1, starting transfers between devices, share_with(): return lax.all_to_all(copies, axes, 0, 0, tiled=True)  6.15 us
    all_to_all x1, waiting for transfers between devices, share_with(): return lax.all_to_all(copies, axes, 0, 0, tiled=True)  3.88 us
    ppermute x1, starting transfers between devices, selection(): got = lax.ppermute(away, 'feat_lo', [(0, 1), (1, 0)])  3.26 us
  transfers between devices with their start and end apart: 3, of which 2 were waited for; matrix products, arithmetic and copies ran while one was open for 1% of the time, Pallas kernels for 0%

profile of v5, /device:TPU:1, one launch (start us, length us, event | category | flops | bytes accessed | tf_op | source)
XLA Modules:
  0.0 108.8 jit_solution(8981241769396444610)
XLA Ops:
  0.6 2.2 %shard_map.49 = f32[16,32,128]{2,1,0:T(8,128)} custom-call(s32[3,32]{1,0:T(4,128)} %bitcast.19, f32[2048,128]{1,0:T(8,128)} %embeddings_hbm.1), custom_call_target="tpu_custom_call" | custom-call | flops 1048576 | bytes 1048576 | tf_op jit(solution)/shard_map/pallas_call | solution.py:70
  2.8 0.0 copy-start
  2.8 21.6 %all_to_all.25 = f32[16,32,128]{2,1,0:T(8,128)S(1)} all-to-all(f32[16,32,128]{2,1,0:T(8,128)} %shard_map.49), channel_id=1, replica_groups=mesh['cand_0'=4,'cand_1'=2,'blk'=8,'feat_hi'=4,'feat_lo'=2] {'cand_1','b..., dimensions={0} | all-to-all | bytes 524288 | tf_op jit(solution)/shard_map/all_to_all | solution.py:82
  24.4 0.7 broadcast_in_dim.6
  25.2 6.1 %all-to-all-start.1 = ((f32[16,32,128]{2,1,0:T(8,128)}), f32[16,32,128]{2,1,0:T(8,128)S(1)}, u32[]{:S(2)}, u32[]{:S(2)}) async-start(f32[16,32,128]{2,1,0:T(8,128)} %broadcast_in_dim.6), calls=%async_computation.1 | async-start | bytes 524288 | tf_op jit(solution)/shard_map/all_to_all | solution.py:33
  31.3 0.0 copy-done
  31.3 0.1 constant_dynamic-slice_fusion
  31.4 3.3 %collective-permute-start = (f32[1024,128]{1,0:T(8,128)S(1)}, f32[1024,128]{1,0:T(8,128)S(1)}, u32[]{:S(2)}, u32[]{:S(2)}) collective-permute-start(f32[1024,128]{1,0:T(8,128)S(1)} %get-tuple-element.7), channel_id=1, source_target_pairs={{0,1},{1,0},{2,3},{3,2},{4,5},{5,4},{6,7},{7,6},{8,9},{9,8},{10,11... | collective-permute-start | bytes 1572872 | tf_op jit(solution)/shard_map/ppermute | solution.py:206
  34.7 3.9 %all-to-all-done.1 = f32[16,32,128]{2,1,0:T(8,128)S(1)} async-done(((f32[16,32,128]{2,1,0:T(8,128)}), f32[16,32,128]{2,1,0:T(8,128)S(1)}, u32[]{:S(2)}, u32[]{:S(2)}) %all-to-all-start.1) | async-done | bytes 262176 | tf_op jit(solution)/shard_map/all_to_all | solution.py:33
  38.7 8.9 %collective-permute-done.got_ref = f32[1024,128]{1,0:T(8,128)S(1)} collective-permute-done((f32[1024,128]{1,0:T(8,128)S(1)}, f32[1024,128]{1,0:T(8,128)S(1)}, u32[]{:S(2)}, u32[]{:S(2)}) %collective-permute-start) | collective-permute-done | bytes 524320 | tf_op jit(solution)/shard_map/ppermute | solution.py:206
  47.6 1.2 %shard_map.50 = f32[4,200,128]{2,1,0:T(8,128)S(1)} custom-call(s32[1]{0:T(128)} %bitcast.side_ref, f32[2,96,128]{2,1,0:T(8,128)S(1)} %bitcast.15, f32[1024,128]{1,0:T(8,128)S(1)} %get-tuple-element.8.mine_ref, f32[1024,128]{1,0:T(8,128)S(1)} %collective-permute-done.got_ref), custom_call_target="tpu_custom_call" | custom-call | flops 50331648 | bytes 2097152 | tf_op jit(solution)/shard_map/pallas_call | solution.py:209
  48.8 17.8 %all_to_all.26.parts_ref = f32[4,200,128]{2,1,0:T(8,128)S(1)} all-to-all(f32[4,200,128]{2,1,0:T(8,128)S(1)} %shard_map.50), channel_id=1, replica_groups=mesh['cand_0'=4,'cand_1'=2,'blk'=8,'feat_hi'=4,'feat_lo'=2] {'feat_hi'}, dimensions={0} | all-to-all | bytes 819200 | tf_op jit(solution)/shard_map/all_to_all | solution.py:217
  66.5 0.2 shard_map.51
  66.7 15.9 %all_to_all.27.own_ref = f32[4,200,128]{2,1,0:T(8,128)S(1)} all-to-all(f32[4,200,128]{2,1,0:T(8,128)S(1)} %shard_map.51), channel_id=1, replica_groups=mesh['cand_0'=4,'cand_1'=2,'blk'=8,'feat_hi'=4,'feat_lo'=2] {'feat_hi'}, dimensions={0} | all-to-all | bytes 819200 | tf_op jit(solution)/shard_map/all_to_all | solution.py:226
  82.7 1.9 %collective-permute-start.1 = (f32[4,200,128]{2,1,0:T(8,128)S(1)}, f32[4,200,128]{2,1,0:T(8,128)S(1)}, u32[]{:S(2)}, u32[]{:S(2)}) collective-permute-start(f32[4,200,128]{2,1,0:T(8,128)S(1)} %all_to_all.27.own_ref), channel_id=1, source_target_pairs={{0,1},{1,0},{2,3},{3,2},{4,5},{5,4},{6,7},{7,6},{8,9},{9,8},{10,11... | collective-permute-start | bytes 1228808 | tf_op jit(solution)/shard_map/ppermute | solution.py:227
  84.7 22.4 %all_to_all.28 = f32[128,1,128]{2,1,0:T(1,128)S(1)} all-to-all(f32[128,1,128]{2,1,0:T(1,128)S(1)} %broadcast_in_dim.7), channel_id=1, replica_groups=mesh['cand_0'=4,'cand_1'=2,'blk'=8,'feat_hi'=4,'feat_lo'=2] {'cand_0','c..., dimensions={0} | all-to-all | bytes 131072 | tf_op jit(solution)/shard_map/all_to_all | solution.py:33
  107.1 0.7 reshape.48
  107.7 0.0 collective-permute-done.1.other_ref
  107.7 1.1 shard_map.52
  (10 shorter events, 0.2 us)
Async XLA Ops:
  2.8 28.5 %copy-start = (f32[2048,128]{1,0:T(8,128)S(1)}, f32[2048,128]{1,0:T(8,128)}, u32[]{:S(2)}) copy-start(f32[2048,128]{1,0:T(8,128)} %embeddings_hbm.1) | copy-start | bytes 3145732
  25.2 13.4 %all-to-all-start.1 = ((f32[16,32,128]{2,1,0:T(8,128)}), f32[16,32,128]{2,1,0:T(8,128)S(1)}, u32[]{:S(2)}, u32[]{:S(2)}) async-start(f32[16,32,128]{2,1,0:T(8,128)} %broadcast_in_dim.6), calls=%async_computation.1 | async-start | bytes 524288 | tf_op jit(solution)/shard_map/all_to_all | solution.py:33
  31.4 16.2 %collective-permute-start = (f32[1024,128]{1,0:T(8,128)S(1)}, f32[1024,128]{1,0:T(8,128)S(1)}, u32[]{:S(2)}, u32[]{:S(2)}) collective-permute-start(f32[1024,128]{1,0:T(8,128)S(1)} %get-tuple-element.7), channel_id=1, source_target_pairs={{0,1},{1,0},{2,3},{3,2},{4,5},{5,4},{6,7},{7,6},{8,9},{9,8},{10,11... | collective-permute-start | bytes 1572872 | tf_op jit(solution)/shard_map/ppermute | solution.py:206
  82.7 25.1 %collective-permute-start.1 = (f32[4,200,128]{2,1,0:T(8,128)S(1)}, f32[4,200,128]{2,1,0:T(8,128)S(1)}, u32[]{:S(2)}, u32[]{:S(2)}) collective-permute-start(f32[4,200,128]{2,1,0:T(8,128)S(1)} %all_to_all.27.own_ref), channel_id=1, source_target_pairs={{0,1},{1,0},{2,3},{3,2},{4,5},{5,4},{6,7},{7,6},{8,9},{9,8},{10,11... | collective-permute-start | bytes 1228808 | tf_op jit(solution)/shard_map/ppermute | solution.py:227
